TPU v7x, 32 devices: a whole 2x2x4 slice. The times are simulated.
32 devices in a mesh: dp: 8 (over z, y), tensor: 4 (over x, core).
Axes of the slice: x: 2, y: 2, z: 4, core: 2. Of those that a mesh axis runs over, the one named last changes fastest.
Arguments:
- tokens_in: bfloat16 [1024, 4096], P(('dp', 'tensor')), may hold values from -6 to 6
- grad_out: bfloat16 [1024, 4096], P(('dp', 'tensor')), may hold values from -6 to 6
- gate_pre: bfloat16 [1024, 7168], P('dp', 'tensor'), may hold values from -6 to 6
- up_pre: bfloat16 [1024, 7168], P('dp', 'tensor'), may hold values from -6 to 6
- gate_weight: bfloat16 [4096, 7168], P('dp', 'tensor'), may hold values from -0.09375 to 0.09375
- up_weight: bfloat16 [4096, 7168], P('dp', 'tensor'), may hold values from -0.09375 to 0.09375
- down_weight: bfloat16 [7168, 4096], P('tensor', 'dp'), may hold values from -0.0625 to 0.0625
- norm_gain: float32 [4096], replicated, may hold values from 0.1 to 1.9
Outputs:
- input_grad: bfloat16 [1024, 4096], P(('dp', 'tensor'))
- gain_grad: float32 [4096], replicated
- down_grad: bfloat16 [7168, 4096], P('tensor', 'dp')
All inputs are finite; a program needn't handle non-finite values.
Results may differ from a plain program's by a relative error of at most 0.015.
Values may be sent and summed in bfloat16 or wider, within the bound.
No kernel may reach another device: no remote copies, remote signals or barrier semaphores. Data moves between devices by JAX's collectives and lax.ppermute only.
A program may use at most 64 MiB of HBM per device.

v0:
```python
import jax
import jax.numpy as jnp
from jax import lax
from jax.sharding import PartitionSpec as P


BF16, F32 = jnp.bfloat16, jnp.float32


def make_per_device(mesh):
    groups, width = mesh.shape["dp"], mesh.shape["tensor"]
    na, nr = groups // 2, width // 2

    def ring(k):
        return [(a * 2 + b, (a + k) % na * 2 + b) for a in range(na) for b in range(2)]

    def move_a(value, k):
        return lax.ppermute(value, "dp", ring(k % na))

    def move_core(value):
        return lax.ppermute(value, "tensor", [(t, t ^ 1) for t in range(width)])

    def move_pair(value):
        return lax.ppermute(value, "dp", [(d, d ^ 1) for d in range(groups)])

    def move_br(value, kb, kr):
        pairs = []
        for d in range(groups):
            for r in range(nr):
                for c in range(2):
                    pairs.append(
                        (d * width + r * 2 + c, (d ^ kb) * width + (r + kr) % nr * 2 + c)
                    )
        return lax.ppermute(value, ("dp", "tensor"), pairs)

    def per_device(
        tokens_in, grad_out, gate_pre, up_pre, gate_weight, up_weight, down_weight, norm_gain
    ):
        rows, features = grad_out.shape
        hidden = gate_pre.shape[1] // 2
        own = down_weight.shape[1]
        pair = own * 2
        group = rows * width
        data, tensor = lax.axis_index("dp"), lax.axis_index("tensor")
        a, b = data // 2, data % 2
        r, c = tensor // 2, tensor % 2
        first = b == 0

        def block_of(value, k):
            return lax.dynamic_slice_in_dim(value, (a + k) % na * pair, pair, 1)

        def ordered(kept, given, axis):
            return jnp.where(
                first,
                jnp.concatenate((kept, given), axis=axis),
                jnp.concatenate((given, kept), axis=axis),
            )

        def halves(value):
            low, high = value[..., :hidden], value[..., hidden:]
            return jnp.where(first, low, high), jnp.where(first, high, low)

        def relative_rows(value):
            blocks = value.reshape(width, rows, value.shape[1])
            return jnp.concatenate(
                [
                    lax.dynamic_index_in_dim(blocks, (r - kr + nr) % nr * 2 + (c ^ kc), 0, False)
                    for kr in range(nr)
                    for kc in range(2)
                ]
            )

        gate_keep, gate_give = halves(relative_rows(gate_pre))
        up_keep, up_give = halves(relative_rows(up_pre))
        pre = [[jnp.stack((gate_keep, up_keep)), move_pair(jnp.stack((gate_give, up_give)))]]

        down_rows = down_weight.reshape(2, hidden, own)
        down_keep = lax.dynamic_index_in_dim(down_rows, b, 0, False)
        down_give = lax.dynamic_index_in_dim(down_rows, 1 - b, 0, False)
        down_pair = ordered(down_keep, move_pair(down_give), 1)

        inputs = tokens_in.astype(F32)
        inv_rms = lax.rsqrt(jnp.mean(inputs * inputs, axis=1, keepdims=True) + 1e-05)
        normed = inputs * inv_rms
        terms, rest = [], inv_rms
        for _ in range(3):
            terms.append(lax.reduce_precision(rest, 8, 7))
            rest = rest - terms[-1]
        extra = jnp.concatenate(terms + [jnp.zeros((rows, 125), F32)], axis=1).astype(BF16)

        near = jnp.stack(
            [move_a(block_of(grad_out, k), k) if k else block_of(grad_out, 0) for k in range(na)]
        )
        every_out = []
        for kb in range(2):
            mine = jnp.stack(
                [near if kb == 0 and kr == 0 else move_br(near, kb, kr) for kr in range(nr)]
            )
            both = jnp.stack((mine, move_core(mine)))
            every_out.append(both.transpose(2, 1, 0, 3, 4).reshape(na, group, pair))

        near_normed = []
        for k in range(na):
            message = jnp.concatenate((block_of(tokens_in, k), extra), axis=1)
            if k:
                message = move_a(message, k)
            near_normed.append(message)

        gate_w_keep, gate_w_give = halves(gate_weight)
        up_w_keep, up_w_give = halves(up_weight)
        weight_keep = jnp.stack((gate_w_keep, up_w_keep))
        weight_give = move_pair(jnp.stack((gate_w_give, up_w_give)))
        weight_pair = jnp.zeros((2, pair, hidden), BF16)
        weight_pair = lax.dynamic_update_slice_in_dim(weight_pair, weight_keep, b * own, 1)
        weight_pair = lax.dynamic_update_slice_in_dim(weight_pair, weight_give, (1 - b) * own, 1)

        for _ in range(1, na):
            pre.append([move_a(pre[-1][kb], 1) for kb in range(2)])

        grads = [[None, None] for _ in range(na)]
        for kb in range(2):
            partial = lax.dot_general(
                every_out[kb].reshape(na * group, pair),
                down_pair,
                (((1,), (1,)), ((), ())),
                preferred_element_type=F32,
            ).astype(BF16).reshape(na, group, hidden)
            running = partial[1]
            for step in range(1, na):
                running = (
                    move_a(running, 1).astype(F32)
                    + partial[(step + 1) % na].astype(F32)
                ).astype(BF16)
            grads[0][kb] = running
            for k in range(1, na):
                grads[k][kb] = move_a(grads[k - 1][kb], 1)

        acts, norm_blocks = [], []
        gain_part = jnp.zeros((pair,), F32)
        for k in range(na):
            value = jnp.concatenate(pre[k], axis=1).astype(F32)
            gate_value, up_value = value[0], value[1]
            gate_sigmoid = jax.nn.sigmoid(gate_value)
            gate_silu = gate_value * gate_sigmoid
            acts.append((gate_silu * up_value).astype(BF16))
            grad_act = jnp.concatenate(grads[k]).astype(F32)
            grad_gate = (
                grad_act * up_value * gate_sigmoid * (1.0 + gate_value * (1.0 - gate_sigmoid))
            ).astype(BF16)
            grad_up = (grad_act * gate_silu).astype(BF16)
            norm_part = jnp.einsum(
                "grf,gdf->rd",
                jnp.stack((grad_gate, grad_up)),
                weight_pair,
                preferred_element_type=F32,
            ).astype(BF16)
            norm_part = norm_part.reshape(2, nr, 2, rows, pair)
            across = move_core(norm_part[:, :, 1])
            cores = (norm_part[:, :, 0].astype(F32) + across.astype(F32)).astype(BF16)
            total = cores[0, 0].astype(F32)
            for kb in range(2):
                for kr in range(nr):
                    if kb or kr:
                        piece = cores[kb, kr]
                        piece = move_br(piece, kb, -kr)
                        total = total + piece.astype(F32)
            message, total = lax.optimization_barrier((near_normed[k], total))
            tail = message[:, pair:].astype(F32)
            their_inputs = message[:, :pair]
            their_inv = tail[:, 0:1] + tail[:, 1:2] + tail[:, 2:3]
            their_normed = their_inputs.astype(F32) * their_inv
            gain_part = gain_part + jnp.sum(total * their_normed, axis=0)
            total = total.astype(BF16)
            norm_blocks.append(move_a(total, -k) if k else total)

        down_both = lax.dot_general(
            jnp.concatenate(acts),
            jnp.concatenate(every_out, axis=1).reshape(na * 2 * group, pair),
            (((0,), (0,)), ((), ())),
            preferred_element_type=F32,
        ).astype(BF16)
        low, high = down_both[:, :own], down_both[:, own:]
        theirs = move_pair(jnp.where(first, high, low))
        down_grad = jnp.zeros((2 * hidden, own), BF16)
        mine = jnp.where(first, low, high)
        down_grad = lax.dynamic_update_slice_in_dim(down_grad, mine, b * hidden, 0)
        down_grad = lax.dynamic_update_slice_in_dim(down_grad, theirs, (1 - b) * hidden, 0)

        gain = gain_part + move_core(gain_part)
        gain_sum = gain
        for kb in range(2):
            for kr in range(nr):
                if kb or kr:
                    gain_sum = gain_sum + move_br(gain, kb, kr)

        def natural(blocks, axis):
            twice = jnp.concatenate(blocks + blocks, axis=axis)
            return lax.dynamic_slice_in_dim(twice, (na - a) % na * pair, features, axis)

        gain_grad = natural([move_a(gain_sum, -k) if k else gain_sum for k in range(na)], 0)
        grad_norm = natural(norm_blocks, 1).astype(F32)
        scaled = grad_norm * norm_gain
        inner = jnp.mean(scaled * normed, axis=1, keepdims=True)
        input_grad = (grad_out.astype(F32) + inv_rms * (scaled - normed * inner)).astype(BF16)
        return (input_grad, gain_grad, down_grad)

    return per_device


def solution(mesh):
    inner = make_per_device(mesh)

    return jax.shard_map(
        inner,
        mesh=mesh,
        in_specs=(
            P(("dp", "tensor"), None),
            P(("dp", "tensor"), None),
            P("dp", "tensor"),
            P("dp", "tensor"),
            P("dp", "tensor"),
            P("dp", "tensor"),
            P("tensor", "dp"),
            P(),
        ),
        out_specs=(P(("dp", "tensor"), None), P(), P("tensor", "dp")),
        check_vma=False,
    )
```

profile of v0, /device:TPU:0, one launch (start us, length us, event | category | flops | bytes accessed | tf_op | source)
XLA Modules:
  0.0 285.8 jit_solution(10811046774975967304)
XLA Ops:
  0.6 2.3 select_bitcast_fusion
  3.0 1.4 pad_maximum_fusion.1
  4.4 3.0 %collective-permute-start.16 = (bf16[2,512,896]{2,1,0:T(8,128)(2,1)}, bf16[2,512,896]{2,1,0:T(8,128)(2,1)}, u32[]{:S(2)}, u32[]{:S(2)}) collective-permute-start(bf16[2,512,896]{2,1,0:T(8,128)(2,1)} %pad_maximum_fusion.1), channel_id=1, source_target_pairs={{0,4},{4,0},{8,12},{12,8},{16,20},{20,16},{24,28},{28,24},{1,5},{5... | collective-permute-start | bytes 5505032 | tf_op jit(solution)/shard_map/ppermute | solution.py:24
  9.2 3.6 %collective-permute-start.2 = (bf16[32,1024]{1,0:T(8,128)(2,1)}, bf16[32,1024]{1,0:T(8,128)(2,1)S(1)}, u32[]{:S(2)}, u32[]{:S(2)}) collective-permute-start(bf16[32,1024]{1,0:T(8,128)(2,1)} %get-tuple-element.75), channel_id=1, source_target_pairs={{0,24},{4,28},{8,0},{12,4},{16,8},{20,12},{24,16},{28,20},{1,25},{... | collective-permute-start | bytes 196616 | tf_op jit(solution)/shard_map/ppermute | solution.py:18
  14.0 2.8 dynamic-slice_bitcast_fusion.1
  16.8 2.4 collective-permute-done.1
  19.8 1.7 fusion.94
  21.5 2.1 collective-permute-start.10
  24.5 2.1 broadcast_in_dim.13
  26.5 1.4 maximum_dynamic-update-slice_fusion
  30.6 1.2 collective-permute-start.5
  31.8 37.9 %collective-permute-done.9 = bf16[4,32,1024]{2,1,0:T(8,128)(2,1)} collective-permute-done((bf16[4,32,1024]{2,1,0:T(8,128)(2,1)}, bf16[4,32,1024]{2,1,0:T(8,128)(2,1)}, u32[]{:S(2)}, u32[]{:S(2)}) %collective-permute-start.9) | collective-permute-done | bytes 262176 | tf_op jit(solution)/shard_map/ppermute | solution.py:34
  69.7 2.1 collective-permute-start.24
  73.6 1.1 maximum_convert_fusion
  75.6 1.6 collective-permute-start.21
  77.4 5.7 %collective-permute-done.24 = bf16[2,128,896]{2,1,0:T(8,128)(2,1)S(1)} collective-permute-done((bf16[2,128,896]{2,1,0:T(8,128)(2,1)S(1)}, bf16[2,128,896]{2,1,0:T(8,128)(2,1)S(1)}, u32[]{:S(2)}, u32[]{:S(2)}) %collective-permute-start.24) | collective-permute-done | bytes 458784 | tf_op jit(solution)/shard_map/ppermute | solution.py:18
  83.1 2.3 collective-permute-start.34
  85.7 2.7 collective-permute-done.5
  88.4 1.3 convolution_convert_fusion
  89.7 1.9 collective-permute-start.12
  91.6 1.3 convolution_convert_fusion.1
  92.9 5.6 %collective-permute-done.25 = bf16[2,128,896]{2,1,0:T(8,128)(2,1)S(1)} collective-permute-done((bf16[2,128,896]{2,1,0:T(8,128)(2,1)}, bf16[2,128,896]{2,1,0:T(8,128)(2,1)S(1)}, u32[]{:S(2)}, u32[]{:S(2)}) %collective-permute-start.25) | collective-permute-done | bytes 458784 | tf_op jit(solution)/shard_map/ppermute | solution.py:18
  98.9 14.4 %collective-permute-done.12 = bf16[128,896]{1,0:T(8,128)(2,1)S(1)} collective-permute-done((bf16[128,896]{1,0:T(8,128)(2,1)S(1)}, bf16[128,896]{1,0:T(8,128)(2,1)S(1)}, u32[]{:S(2)}, u32[]{:S(2)}) %collective-permute-start.12) | collective-permute-done | bytes 229408 | tf_op jit(solution)/shard_map/ppermute | solution.py:18
  113.4 1.5 collective-permute-start.31
  114.9 3.4 %collective-permute-done.6 = bf16[128,896]{1,0:T(8,128)(2,1)S(1)} collective-permute-done((bf16[128,896]{1,0:T(8,128)(2,1)S(1)}, bf16[128,896]{1,0:T(8,128)(2,1)S(1)}, u32[]{:S(2)}, u32[]{:S(2)}) %collective-permute-start.6) | collective-permute-done | bytes 229408 | tf_op jit(solution)/shard_map/ppermute | solution.py:18
  118.3 10.3 %collective-permute-done.35 = bf16[2,128,896]{2,1,0:T(8,128)(2,1)S(1)} collective-permute-done((bf16[2,128,896]{2,1,0:T(8,128)(2,1)S(1)}, bf16[2,128,896]{2,1,0:T(8,128)(2,1)S(1)}, u32[]{:S(2)}, u32[]{:S(2)}) %collective-permute-start.35) | collective-permute-done | bytes 458784 | tf_op jit(solution)/shard_map/ppermute | solution.py:18
  129.0 11.4 %collective-permute-done.13 = bf16[128,896]{1,0:T(8,128)(2,1)S(1)} collective-permute-done((bf16[128,896]{1,0:T(8,128)(2,1)S(1)}, bf16[128,896]{1,0:T(8,128)(2,1)S(1)}, u32[]{:S(2)}, u32[]{:S(2)}) %collective-permute-start.13) | collective-permute-done | bytes 229408 | tf_op jit(solution)/shard_map/ppermute | solution.py:18
  141.3 8.6 %collective-permute-done.7 = bf16[128,896]{1,0:T(8,128)(2,1)S(1)} collective-permute-done((bf16[128,896]{1,0:T(8,128)(2,1)S(1)}, bf16[128,896]{1,0:T(8,128)(2,1)S(1)}, u32[]{:S(2)}, u32[]{:S(2)}) %collective-permute-start.7) | collective-permute-done | bytes 229408 | tf_op jit(solution)/shard_map/ppermute | solution.py:18
  149.9 9.9 %collective-permute-done.14 = bf16[128,896]{1,0:T(8,128)(2,1)S(1)} collective-permute-done((bf16[128,896]{1,0:T(8,128)(2,1)S(1)}, bf16[128,896]{1,0:T(8,128)(2,1)S(1)}, u32[]{:S(2)}, u32[]{:S(2)}) %collective-permute-start.14) | collective-permute-done | bytes 229408 | tf_op jit(solution)/shard_map/ppermute | solution.py:18
  159.9 10.2 %collective-permute-done.8 = bf16[128,896]{1,0:T(8,128)(2,1)S(1)} collective-permute-done((bf16[128,896]{1,0:T(8,128)(2,1)S(1)}, bf16[128,896]{1,0:T(8,128)(2,1)S(1)}, u32[]{:S(2)}, u32[]{:S(2)}) %collective-permute-start.8) | collective-permute-done | bytes 229408 | tf_op jit(solution)/shard_map/ppermute | solution.py:18
  170.8 2.9 %constant_dynamic-update-slice_fusion.15 = bf16[2,1024,896]{2,1,0:T(8,128)(2,1)} fusion(bf16[2,1024,896]{2,1,0:T(8,128)(2,1)} %maximum_dynamic-update-slice_fusion, bf16[2,512,896]{2,1,0:T(8,128)(2,1)} %collective-permute-done.16, s32[]{:T(128)S(6)} %select_n.217), kind=kLoop, calls=%fused_computation.230 | loop fusion | bytes 3670020 | tf_op jit(solution)/shard_map/dynamic_update_slice | solution.py:115
  173.7 3.2 %fusion.11 = bf16[256,1024]{1,0:T(8,128)(2,1)S(1)} fusion(bf16[2,1024,896]{2,1,0:T(8,128)(2,1)} %constant_dynamic-update-slice_fusion.15, bf16[1,256,896]{2,1,0:T(8,128)(2,1)S(1)} %get-tuple-element.30, bf16[1,256,896]{2,1,0:T(8,128)(2,1)S(1)} %get-tuple-element.29), kind=kOutput, calls=%fused_computation.19 | convolution fusion | flops 940244992 | bytes 5111808 | tf_op jit(solution)/shard_map/grf,gdf->rd/dot_general | solution.py:151
  177.8 3.4 %collective-permute-done.45 = bf16[2,128,896]{2,1,0:T(8,128)(2,1)S(1)} collective-permute-done((bf16[2,128,896]{2,1,0:T(8,128)(2,1)S(1)}, bf16[2,128,896]{2,1,0:T(8,128)(2,1)S(1)}, u32[]{:S(2)}, u32[]{:S(2)}) %collective-permute-start.45) | collective-permute-done | bytes 458784 | tf_op jit(solution)/shard_map/ppermute | solution.py:18
  181.6 2.0 collective-permute-done.23
  183.7 2.5 collective-permute-done.22
  186.7 3.2 %fusion.12 = bf16[256,1024]{1,0:T(8,128)(2,1)S(1)} fusion(bf16[2,1024,896]{2,1,0:T(8,128)(2,1)} %constant_dynamic-update-slice_fusion.15, bf16[1,256,896]{2,1,0:T(8,128)(2,1)S(1)} %get-tuple-element.28, bf16[1,256,896]{2,1,0:T(8,128)(2,1)S(1)} %get-tuple-element.27), kind=kOutput, calls=%fused_computation.20 | convolution fusion | flops 940244992 | bytes 5111808 | tf_op jit(solution)/shard_map/grf,gdf->rd/dot_general | solution.py:151
  189.9 2.1 fusion.8
  192.7 2.0 collective-permute-start.32
  194.7 5.8 %collective-permute-done.33 = bf16[128,896]{1,0:T(8,128)(2,1)S(1)} collective-permute-done((bf16[128,896]{1,0:T(8,128)(2,1)S(1)}, bf16[128,896]{1,0:T(8,128)(2,1)S(1)}, u32[]{:S(2)}, u32[]{:S(2)}) %collective-permute-start.33) | collective-permute-done | bytes 229408 | tf_op jit(solution)/shard_map/ppermute | solution.py:18
  200.5 2.5 collective-permute-done.32
  203.5 3.2 %fusion.13 = bf16[256,1024]{1,0:T(8,128)(2,1)S(1)} fusion(bf16[2,1024,896]{2,1,0:T(8,128)(2,1)} %constant_dynamic-update-slice_fusion.15, bf16[1,256,896]{2,1,0:T(8,128)(2,1)S(1)} %get-tuple-element.26, bf16[1,256,896]{2,1,0:T(8,128)(2,1)S(1)} %get-tuple-element.25), kind=kOutput, calls=%fused_computation.21 | convolution fusion | flops 940244992 | bytes 5111808 | tf_op jit(solution)/shard_map/grf,gdf->rd/dot_general | solution.py:151
  206.8 2.3 collective-permute-start.20
  210.5 1.6 collective-permute-done.20
  212.1 2.3 collective-permute-start.29
  215.0 1.2 collective-permute-start.27
  217.3 1.4 collective-permute-done.28
  220.4 9.2 %collective-permute-done.43 = bf16[128,896]{1,0:T(8,128)(2,1)S(1)} collective-permute-done((bf16[128,896]{1,0:T(8,128)(2,1)S(1)}, bf16[128,896]{1,0:T(8,128)(2,1)S(1)}, u32[]{:S(2)}, u32[]{:S(2)}) %collective-permute-start.43) | collective-permute-done | bytes 229408 | tf_op jit(solution)/shard_map/ppermute | solution.py:18
  229.6 3.8 %collective-permute-done.42 = bf16[128,896]{1,0:T(8,128)(2,1)S(1)} collective-permute-done((bf16[128,896]{1,0:T(8,128)(2,1)S(1)}, bf16[128,896]{1,0:T(8,128)(2,1)S(1)}, u32[]{:S(2)}, u32[]{:S(2)}) %collective-permute-start.42) | collective-permute-done | bytes 229408 | tf_op jit(solution)/shard_map/ppermute | solution.py:18
  234.0 3.2 %fusion.14 = bf16[256,1024]{1,0:T(8,128)(2,1)S(1)} fusion(bf16[2,1024,896]{2,1,0:T(8,128)(2,1)} %constant_dynamic-update-slice_fusion.15, bf16[1,256,896]{2,1,0:T(8,128)(2,1)S(1)} %get-tuple-element.24, bf16[1,256,896]{2,1,0:T(8,128)(2,1)S(1)} %get-tuple-element.23), kind=kOutput, calls=%fused_computation.22 | convolution fusion | flops 940244992 | bytes 5111808 | tf_op jit(solution)/shard_map/grf,gdf->rd/dot_general | solution.py:151
  237.3 1.7 collective-permute-start.39
  239.5 1.4 collective-permute-start.37
  240.9 2.3 collective-permute-done.39
  244.3 1.3 collective-permute-done.46
  246.8 1.3 collective-permute-start.48
  248.0 1.2 collective-permute-start.47
  249.3 2.1 collective-permute-done.49
  251.4 14.6 %collective-permute-done.48 = bf16[32,1024]{1,0:T(8,128)(2,1)S(1)} collective-permute-done((bf16[32,1024]{1,0:T(8,128)(2,1)S(1)}, bf16[32,1024]{1,0:T(8,128)(2,1)S(1)}, u32[]{:S(2)}, u32[]{:S(2)}) %collective-permute-start.48) | collective-permute-done | bytes 65568 | tf_op jit(solution)/shard_map/ppermute | solution.py:34
  266.5 1.1 collective-permute-done.51
  267.7 1.3 collective-permute-start.54
  269.6 1.6 collective-permute-start.52
  273.2 3.2 %collective-permute-done.40 = bf16[32,1024]{1,0:T(8,128)(2,1)S(1)} collective-permute-done((bf16[32,1024]{1,0:T(8,128)(2,1)S(1)}, bf16[32,1024]{1,0:T(8,128)(2,1)S(1)}, u32[]{:S(2)}, u32[]{:S(2)}) %collective-permute-start.40) | collective-permute-done | bytes 65568 | tf_op jit(solution)/shard_map/ppermute | solution.py:18
  277.1 3.7 %collective-permute-start.57 = (f32[1024]{0:T(1024)S(1)}, f32[1024]{0:T(1024)S(1)}, u32[]{:S(2)}, u32[]{:S(2)}) collective-permute-start(f32[1024]{0:T(1024)S(1)} %get-tuple-element.20), channel_id=1, source_target_pairs={{0,8},{4,12},{8,16},{12,20},{16,24},{20,28},{24,0},{28,4},{1,9},{5... | collective-permute-start | bytes 12296 | tf_op jit(solution)/shard_map/ppermute | solution.py:18
  281.0 1.6 collective-permute-done.57
  284.6 1.2 copy-done.1
  (193 shorter events, 29.9 us)
Async XLA Ops:
  3.0 4.4 %copy-start.5 = (bf16[128,1792]{1,0:T(8,128)(2,1)S(1)}, bf16[128,1792]{1,0:T(8,128)(2,1)}, u32[]{:S(2)}) copy-start(bf16[128,1792]{1,0:T(8,128)(2,1)} %param.11) | copy-start | bytes 1376260
  3.0 4.5 %copy-start.6 = (bf16[128,1792]{1,0:T(8,128)(2,1)S(1)}, bf16[128,1792]{1,0:T(8,128)(2,1)}, u32[]{:S(2)}) copy-start(bf16[128,1792]{1,0:T(8,128)(2,1)} %param.10) | copy-start | bytes 1376260
  4.4 166.3 %collective-permute-start.16 = (bf16[2,512,896]{2,1,0:T(8,128)(2,1)}, bf16[2,512,896]{2,1,0:T(8,128)(2,1)}, u32[]{:S(2)}, u32[]{:S(2)}) collective-permute-start(bf16[2,512,896]{2,1,0:T(8,128)(2,1)} %pad_maximum_fusion.1), channel_id=1, source_target_pairs={{0,4},{4,0},{8,12},{12,8},{16,20},{20,16},{24,28},{28,24},{1,5},{5... | collective-permute-start | bytes 5505032 | tf_op jit(solution)/shard_map/ppermute | solution.py:24
  7.6 6.2 %copy-start = (bf16[32,4096]{1,0:T(8,128)(2,1)S(1)}, bf16[32,4096]{1,0:T(8,128)(2,1)}, u32[]{:S(2)}) copy-start(bf16[32,4096]{1,0:T(8,128)(2,1)} %param.8) | copy-start | bytes 786436
  7.8 65.2 %collective-permute-start.15 = (bf16[2,128,896]{2,1,0:T(8,128)(2,1)S(1)}, bf16[2,128,896]{2,1,0:T(8,128)(2,1)}, u32[]{:S(2)}, u32[]{:S(2)}) collective-permute-start(bf16[2,128,896]{2,1,0:T(8,128)(2,1)S(1)} %pad_maximum_fusion.9), channel_id=1, source_target_pairs={{0,4},{4,0},{8,12},{12,8},{16,20},{20,16},{24,28},{28,24},{1,5},{5... | collective-permute-start | bytes 1376264 | tf_op jit(solution)/shard_map/ppermute | solution.py:24
  9.2 7.7 %collective-permute-start.2 = (bf16[32,1024]{1,0:T(8,128)(2,1)}, bf16[32,1024]{1,0:T(8,128)(2,1)S(1)}, u32[]{:S(2)}, u32[]{:S(2)}) collective-permute-start(bf16[32,1024]{1,0:T(8,128)(2,1)} %get-tuple-element.75), channel_id=1, source_target_pairs={{0,24},{4,28},{8,0},{12,4},{16,8},{20,12},{24,16},{28,20},{1,25},{... | collective-permute-start | bytes 196616 | tf_op jit(solution)/shard_map/ppermute | solution.py:18
  12.8 6.4 %collective-permute-start.1 = (bf16[32,1024]{1,0:T(8,128)(2,1)}, bf16[32,1024]{1,0:T(8,128)(2,1)S(1)}, u32[]{:S(2)}, u32[]{:S(2)}) collective-permute-start(bf16[32,1024]{1,0:T(8,128)(2,1)} %get-tuple-element.76), channel_id=1, source_target_pairs={{0,16},{4,20},{8,24},{12,28},{16,0},{20,4},{24,8},{28,12},{1,17},{... | collective-permute-start | bytes 196616 | tf_op jit(solution)/shard_map/ppermute | solution.py:18
  12.8 6.4 %collective-permute-start = (bf16[32,1024]{1,0:T(8,128)(2,1)S(1)}, bf16[32,1024]{1,0:T(8,128)(2,1)S(1)}, u32[]{:S(2)}, u32[]{:S(2)}) collective-permute-start(bf16[32,1024]{1,0:T(8,128)(2,1)S(1)} %get-tuple-element.74), channel_id=1, source_target_pairs={{0,8},{4,12},{8,16},{12,20},{16,24},{20,28},{24,0},{28,4},{1,9},{5... | collective-permute-start | bytes 196616 | tf_op jit(solution)/shard_map/ppermute | solution.py:18
  21.5 9.0 %collective-permute-start.10 = (bf16[4,32,1024]{2,1,0:T(8,128)(2,1)}, bf16[4,32,1024]{2,1,0:T(8,128)(2,1)}, u32[]{:S(2)}, u32[]{:S(2)}) collective-permute-start(bf16[4,32,1024]{2,1,0:T(8,128)(2,1)} %get-tuple-element.72), channel_id=1, source_target_pairs={{0,6},{1,7},{2,4},{3,5},{4,2},{5,3},{6,0},{7,1},{8,14},{9,15},{10,... | collective-permute-start | bytes 786440 | tf_op jit(solution)/shard_map/ppermute | solution.py:34
  23.6 46.1 %collective-permute-start.9 = (bf16[4,32,1024]{2,1,0:T(8,128)(2,1)}, bf16[4,32,1024]{2,1,0:T(8,128)(2,1)}, u32[]{:S(2)}, u32[]{:S(2)}) collective-permute-start(bf16[4,32,1024]{2,1,0:T(8,128)(2,1)} %get-tuple-element.72), channel_id=1, source_target_pairs={{0,4},{1,5},{2,6},{3,7},{4,0},{5,1},{6,2},{7,3},{8,12},{9,13},{10,... | collective-permute-start | bytes 786440 | tf_op jit(solution)/shard_map/ppermute | solution.py:34
  27.9 44.9 %collective-permute-start.3 = (bf16[4,32,1024]{2,1,0:T(8,128)(2,1)}, bf16[4,32,1024]{2,1,0:T(8,128)(2,1)S(1)}, u32[]{:S(2)}, u32[]{:S(2)}) collective-permute-start(bf16[4,32,1024]{2,1,0:T(8,128)(2,1)} %get-tuple-element.72), channel_id=1, source_target_pairs={{0,2},{1,3},{2,0},{3,1},{4,6},{5,7},{6,4},{7,5},{8,10},{9,11},{10,... | collective-permute-start | bytes 786440 | tf_op jit(solution)/shard_map/ppermute | solution.py:34
  30.6 57.8 %collective-permute-start.5 = (bf16[896,512]{1,0:T(8,128)(2,1)S(1)}, bf16[896,512]{1,0:T(8,128)(2,1)S(1)}, u32[]{:S(2)}, u32[]{:S(2)}) collective-permute-start(bf16[896,512]{1,0:T(8,128)(2,1)S(1)} %copy-done.4), channel_id=1, source_target_pairs={{0,4},{4,0},{8,12},{12,8},{16,20},{20,16},{24,28},{28,24},{1,5},{5... | collective-permute-start | bytes 2752520 | tf_op jit(solution)/shard_map/ppermute | solution.py:24
  69.7 13.4 %collective-permute-start.24 = (bf16[2,128,896]{2,1,0:T(8,128)(2,1)S(1)}, bf16[2,128,896]{2,1,0:T(8,128)(2,1)S(1)}, u32[]{:S(2)}, u32[]{:S(2)}) collective-permute-start(bf16[2,128,896]{2,1,0:T(8,128)(2,1)S(1)} %pad_maximum_fusion.8), channel_id=1, source_target_pairs={{0,8},{4,12},{8,16},{12,20},{16,24},{20,28},{24,0},{28,4},{1,9},{5... | collective-permute-start | bytes 1376264 | tf_op jit(solution)/shard_map/ppermute | solution.py:18
  72.9 2.2 collective-permute-start.11
  73.0 10.1 %collective-permute-start.4 = (bf16[2,4,32,1024]{3,2,0,1:T(8,128)(2,1)S(1)}, bf16[2,4,32,1024]{3,2,0,1:T(8,128)(2,1)S(1)}, u32[]{:S(2)}, u32[]{:S(2)}) collective-permute-start(bf16[2,4,32,1024]{3,2,0,1:T(8,128)(2,1)S(1)} %get-tuple-element.40), channel_id=1, source_target_pairs={{0,1},{1,0},{2,3},{3,2},{4,5},{5,4},{6,7},{7,6},{8,9},{9,8},{10,11... | collective-permute-start | bytes 1572872 | tf_op jit(solution)/shard_map/ppermute | solution.py:21
  75.6 143.8 %collective-permute-start.21 = (bf16[32,1152]{1,0:T(8,128)(2,1)S(1)}, bf16[32,1152]{1,0:T(8,128)(2,1)S(1)}, u32[]{:S(2)}, u32[]{:S(2)}) collective-permute-start(bf16[32,1152]{1,0:T(8,128)(2,1)S(1)} %copy-done.8), channel_id=1, source_target_pairs={{0,8},{4,12},{8,16},{12,20},{16,24},{20,28},{24,0},{28,4},{1,9},{5... | collective-permute-start | bytes 221192 | tf_op jit(solution)/shard_map/ppermute | solution.py:18
  83.1 15.4 %collective-permute-start.25 = (bf16[2,128,896]{2,1,0:T(8,128)(2,1)}, bf16[2,128,896]{2,1,0:T(8,128)(2,1)S(1)}, u32[]{:S(2)}, u32[]{:S(2)}) collective-permute-start(bf16[2,128,896]{2,1,0:T(8,128)(2,1)} %collective-permute-done.15), channel_id=1, source_target_pairs={{0,8},{4,12},{8,16},{12,20},{16,24},{20,28},{24,0},{28,4},{1,9},{5... | collective-permute-start | bytes 1376264 | tf_op jit(solution)/shard_map/ppermute | solution.py:18
  83.1 30.3 %collective-permute-start.34 = (bf16[2,128,896]{2,1,0:T(8,128)(2,1)S(1)}, bf16[2,128,896]{2,1,0:T(8,128)(2,1)S(1)}, u32[]{:S(2)}, u32[]{:S(2)}) collective-permute-start(bf16[2,128,896]{2,1,0:T(8,128)(2,1)S(1)} %collective-permute-done.24), channel_id=1, source_target_pairs={{0,8},{4,12},{8,16},{12,20},{16,24},{20,28},{24,0},{28,4},{1,9},{5... | collective-permute-start | bytes 1376264 | tf_op jit(solution)/shard_map/ppermute | solution.py:18
  89.7 23.6 %collective-permute-start.12 = (bf16[128,896]{1,0:T(8,128)(2,1)S(1)}, bf16[128,896]{1,0:T(8,128)(2,1)S(1)}, u32[]{:S(2)}, u32[]{:S(2)}) collective-permute-start(bf16[128,896]{1,0:T(8,128)(2,1)S(1)} %slice.292), channel_id=1, source_target_pairs={{0,8},{4,12},{8,16},{12,20},{16,24},{20,28},{24,0},{28,4},{1,9},{5... | collective-permute-start | bytes 688136 | tf_op jit(solution)/shard_map/ppermute | solution.py:18
  98.5 19.8 %collective-permute-start.6 = (bf16[128,896]{1,0:T(8,128)(2,1)S(1)}, bf16[128,896]{1,0:T(8,128)(2,1)S(1)}, u32[]{:S(2)}, u32[]{:S(2)}) collective-permute-start(bf16[128,896]{1,0:T(8,128)(2,1)S(1)} %slice.288), channel_id=1, source_target_pairs={{0,8},{4,12},{8,16},{12,20},{16,24},{20,28},{24,0},{28,4},{1,9},{5... | collective-permute-start | bytes 688136 | tf_op jit(solution)/shard_map/ppermute | solution.py:18
  113.3 15.2 %collective-permute-start.35 = (bf16[2,128,896]{2,1,0:T(8,128)(2,1)S(1)}, bf16[2,128,896]{2,1,0:T(8,128)(2,1)S(1)}, u32[]{:S(2)}, u32[]{:S(2)}) collective-permute-start(bf16[2,128,896]{2,1,0:T(8,128)(2,1)S(1)} %collective-permute-done.25), channel_id=1, source_target_pairs={{0,8},{4,12},{8,16},{12,20},{16,24},{20,28},{24,0},{28,4},{1,9},{5... | collective-permute-start | bytes 1376264 | tf_op jit(solution)/shard_map/ppermute | solution.py:18
  113.4 130.7 %collective-permute-start.31 = (bf16[32,1152]{1,0:T(8,128)(2,1)S(1)}, bf16[32,1152]{1,0:T(8,128)(2,1)S(1)}, u32[]{:S(2)}, u32[]{:S(2)}) collective-permute-start(bf16[32,1152]{1,0:T(8,128)(2,1)S(1)} %concatenate.128), channel_id=1, source_target_pairs={{0,16},{4,20},{8,24},{12,28},{16,0},{20,4},{24,8},{28,12},{1,17},{... | collective-permute-start | bytes 221192 | tf_op jit(solution)/shard_map/ppermute | solution.py:18
  118.3 58.7 %collective-permute-start.44 = (bf16[2,128,896]{2,1,0:T(8,128)(2,1)S(1)}, bf16[2,128,896]{2,1,0:T(8,128)(2,1)S(1)}, u32[]{:S(2)}, u32[]{:S(2)}) collective-permute-start(bf16[2,128,896]{2,1,0:T(8,128)(2,1)S(1)} %collective-permute-done.34), channel_id=1, source_target_pairs={{0,8},{4,12},{8,16},{12,20},{16,24},{20,28},{24,0},{28,4},{1,9},{5... | collective-permute-start | bytes 1376264 | tf_op jit(solution)/shard_map/ppermute | solution.py:18
  128.6 11.8 %collective-permute-start.13 = (bf16[128,896]{1,0:T(8,128)(2,1)S(1)}, bf16[128,896]{1,0:T(8,128)(2,1)S(1)}, u32[]{:S(2)}, u32[]{:S(2)}) collective-permute-start(bf16[128,896]{1,0:T(8,128)(2,1)S(1)} %add_convert_fusion.2), channel_id=1, source_target_pairs={{0,8},{4,12},{8,16},{12,20},{16,24},{20,28},{24,0},{28,4},{1,9},{5... | collective-permute-start | bytes 688136 | tf_op jit(solution)/shard_map/ppermute | solution.py:18
  140.4 9.4 %collective-permute-start.7 = (bf16[128,896]{1,0:T(8,128)(2,1)S(1)}, bf16[128,896]{1,0:T(8,128)(2,1)S(1)}, u32[]{:S(2)}, u32[]{:S(2)}) collective-permute-start(bf16[128,896]{1,0:T(8,128)(2,1)S(1)} %add_convert_fusion.5), channel_id=1, source_target_pairs={{0,8},{4,12},{8,16},{12,20},{16,24},{20,28},{24,0},{28,4},{1,9},{5... | collective-permute-start | bytes 688136 | tf_op jit(solution)/shard_map/ppermute | solution.py:18
  149.8 10.0 %collective-permute-start.14 = (bf16[128,896]{1,0:T(8,128)(2,1)S(1)}, bf16[128,896]{1,0:T(8,128)(2,1)S(1)}, u32[]{:S(2)}, u32[]{:S(2)}) collective-permute-start(bf16[128,896]{1,0:T(8,128)(2,1)S(1)} %add_convert_fusion.1), channel_id=1, source_target_pairs={{0,8},{4,12},{8,16},{12,20},{16,24},{20,28},{24,0},{28,4},{1,9},{5... | collective-permute-start | bytes 688136 | tf_op jit(solution)/shard_map/ppermute | solution.py:18
  159.8 10.3 %collective-permute-start.8 = (bf16[128,896]{1,0:T(8,128)(2,1)S(1)}, bf16[128,896]{1,0:T(8,128)(2,1)S(1)}, u32[]{:S(2)}, u32[]{:S(2)}) collective-permute-start(bf16[128,896]{1,0:T(8,128)(2,1)S(1)} %add_convert_fusion.4), channel_id=1, source_target_pairs={{0,8},{4,12},{8,16},{12,20},{16,24},{20,28},{24,0},{28,4},{1,9},{5... | collective-permute-start | bytes 688136 | tf_op jit(solution)/shard_map/ppermute | solution.py:18
  170.1 11.1 %collective-permute-start.45 = (bf16[2,128,896]{2,1,0:T(8,128)(2,1)S(1)}, bf16[2,128,896]{2,1,0:T(8,128)(2,1)S(1)}, u32[]{:S(2)}, u32[]{:S(2)}) collective-permute-start(bf16[2,128,896]{2,1,0:T(8,128)(2,1)S(1)} %collective-permute-done.35), channel_id=1, source_target_pairs={{0,8},{4,12},{8,16},{12,20},{16,24},{20,28},{24,0},{28,4},{1,9},{5... | collective-permute-start | bytes 1376264 | tf_op jit(solution)/shard_map/ppermute | solution.py:18
  170.7 12.9 %collective-permute-start.23 = (bf16[128,896]{1,0:T(8,128)(2,1)S(1)}, bf16[128,896]{1,0:T(8,128)(2,1)S(1)}, u32[]{:S(2)}, u32[]{:S(2)}) collective-permute-start(bf16[128,896]{1,0:T(8,128)(2,1)S(1)} %add_convert_fusion), channel_id=1, source_target_pairs={{0,8},{4,12},{8,16},{12,20},{16,24},{20,28},{24,0},{28,4},{1,9},{5... | collective-permute-start | bytes 688136 | tf_op jit(solution)/shard_map/ppermute | solution.py:18
  176.9 9.2 %collective-permute-start.22 = (bf16[128,896]{1,0:T(8,128)(2,1)S(1)}, bf16[128,896]{1,0:T(8,128)(2,1)S(1)}, u32[]{:S(2)}, u32[]{:S(2)}) collective-permute-start(bf16[128,896]{1,0:T(8,128)(2,1)S(1)} %add_convert_fusion.3), channel_id=1, source_target_pairs={{0,8},{4,12},{8,16},{12,20},{16,24},{20,28},{24,0},{28,4},{1,9},{5... | collective-permute-start | bytes 688136 | tf_op jit(solution)/shard_map/ppermute | solution.py:18
  181.2 25.5 %collective-permute-start.17 = (bf16[2,2,32,1024]{3,2,1,0:T(8,128)(2,1)S(1)}, bf16[2,2,32,1024]{3,2,1,0:T(8,128)(2,1)S(1)}, u32[]{:S(2)}, u32[]{:S(2)}) collective-permute-start(bf16[2,2,32,1024]{3,2,1,0:T(8,128)(2,1)S(1)} %slice_bitcast_fusion.6), channel_id=1, source_target_pairs={{0,1},{1,0},{2,3},{3,2},{4,5},{5,4},{6,7},{7,6},{8,9},{9,8},{10,11... | collective-permute-start | bytes 786440 | tf_op jit(solution)/shard_map/ppermute | solution.py:21
  192.6 7.9 %collective-permute-start.33 = (bf16[128,896]{1,0:T(8,128)(2,1)S(1)}, bf16[128,896]{1,0:T(8,128)(2,1)S(1)}, u32[]{:S(2)}, u32[]{:S(2)}) collective-permute-start(bf16[128,896]{1,0:T(8,128)(2,1)S(1)} %collective-permute-done.23), channel_id=1, source_target_pairs={{0,8},{4,12},{8,16},{12,20},{16,24},{20,28},{24,0},{28,4},{1,9},{5... | collective-permute-start | bytes 688136 | tf_op jit(solution)/shard_map/ppermute | solution.py:18
  192.7 10.3 %collective-permute-start.32 = (bf16[128,896]{1,0:T(8,128)(2,1)S(1)}, bf16[128,896]{1,0:T(8,128)(2,1)S(1)}, u32[]{:S(2)}, u32[]{:S(2)}) collective-permute-start(bf16[128,896]{1,0:T(8,128)(2,1)S(1)} %collective-permute-done.22), channel_id=1, source_target_pairs={{0,8},{4,12},{8,16},{12,20},{16,24},{20,28},{24,0},{28,4},{1,9},{5... | collective-permute-start | bytes 688136 | tf_op jit(solution)/shard_map/ppermute | solution.py:18
  200.5 9.2 %collective-permute-start.26 = (bf16[2,2,32,1024]{3,2,1,0:T(8,128)(2,1)S(1)}, bf16[2,2,32,1024]{3,2,1,0:T(8,128)(2,1)S(1)}, u32[]{:S(2)}, u32[]{:S(2)}) collective-permute-start(bf16[2,2,32,1024]{3,2,1,0:T(8,128)(2,1)S(1)} %slice_bitcast_fusion.4), channel_id=1, source_target_pairs={{0,1},{1,0},{2,3},{3,2},{4,5},{5,4},{6,7},{7,6},{8,9},{9,8},{10,11... | collective-permute-start | bytes 786440 | tf_op jit(solution)/shard_map/ppermute | solution.py:21
  206.7 13.3 %copy-start.7 = (bf16[32,1152]{1,0:T(8,128)(2,1)S(1)}, bf16[32,1152]{1,0:T(8,128)(2,1)}, u32[]{:S(2)}) copy-start(bf16[32,1152]{1,0:T(8,128)(2,1)} %concatenate.114) | copy-start | bytes 221188
  206.8 5.3 %collective-permute-start.20 = (bf16[32,1024]{1,0:T(8,128)(2,1)S(1)}, bf16[32,1024]{1,0:T(8,128)(2,1)S(1)}, u32[]{:S(2)}, u32[]{:S(2)}) collective-permute-start(bf16[32,1024]{1,0:T(8,128)(2,1)S(1)} %get-tuple-element.69), channel_id=1, source_target_pairs={{0,6},{1,7},{2,4},{3,5},{4,2},{5,3},{6,0},{7,1},{8,14},{9,15},{10,... | collective-permute-start | bytes 196616 | tf_op jit(solution)/shard_map/ppermute | solution.py:34
  209.1 5.3 %collective-permute-start.19 = (bf16[32,1024]{1,0:T(8,128)(2,1)S(1)}, bf16[32,1024]{1,0:T(8,128)(2,1)S(1)}, u32[]{:S(2)}, u32[]{:S(2)}) collective-permute-start(bf16[32,1024]{1,0:T(8,128)(2,1)S(1)} %get-tuple-element.70), channel_id=1, source_target_pairs={{0,4},{1,5},{2,6},{3,7},{4,0},{5,1},{6,2},{7,3},{8,12},{9,13},{10,... | collective-permute-start | bytes 196616 | tf_op jit(solution)/shard_map/ppermute | solution.py:34
  209.7 5.4 %collective-permute-start.18 = (bf16[32,1024]{1,0:T(8,128)(2,1)S(1)}, bf16[32,1024]{1,0:T(8,128)(2,1)S(1)}, u32[]{:S(2)}, u32[]{:S(2)}) collective-permute-start(bf16[32,1024]{1,0:T(8,128)(2,1)S(1)} %get-tuple-element.68), channel_id=1, source_target_pairs={{0,2},{1,3},{2,0},{3,1},{4,6},{5,7},{6,4},{7,5},{8,10},{9,11},{10,... | collective-permute-start | bytes 196616 | tf_op jit(solution)/shard_map/ppermute | solution.py:34
  212.1 5.2 %collective-permute-start.29 = (bf16[32,1024]{1,0:T(8,128)(2,1)S(1)}, bf16[32,1024]{1,0:T(8,128)(2,1)S(1)}, u32[]{:S(2)}, u32[]{:S(2)}) collective-permute-start(bf16[32,1024]{1,0:T(8,128)(2,1)S(1)} %get-tuple-element.66), channel_id=1, source_target_pairs={{0,6},{1,7},{2,4},{3,5},{4,2},{5,3},{6,0},{7,1},{8,14},{9,15},{10,... | collective-permute-start | bytes 196616 | tf_op jit(solution)/shard_map/ppermute | solution.py:34
  214.4 4.3 %collective-permute-start.28 = (bf16[32,1024]{1,0:T(8,128)(2,1)S(1)}, bf16[32,1024]{1,0:T(8,128)(2,1)S(1)}, u32[]{:S(2)}, u32[]{:S(2)}) collective-permute-start(bf16[32,1024]{1,0:T(8,128)(2,1)S(1)} %get-tuple-element.67), channel_id=1, source_target_pairs={{0,4},{1,5},{2,6},{3,7},{4,0},{5,1},{6,2},{7,3},{8,12},{9,13},{10,... | collective-permute-start | bytes 196616 | tf_op jit(solution)/shard_map/ppermute | solution.py:34
  215.0 4.3 %collective-permute-start.27 = (bf16[32,1024]{1,0:T(8,128)(2,1)S(1)}, bf16[32,1024]{1,0:T(8,128)(2,1)S(1)}, u32[]{:S(2)}, u32[]{:S(2)}) collective-permute-start(bf16[32,1024]{1,0:T(8,128)(2,1)S(1)} %get-tuple-element.65), channel_id=1, source_target_pairs={{0,2},{1,3},{2,0},{3,1},{4,6},{5,7},{6,4},{7,5},{8,10},{9,11},{10,... | collective-permute-start | bytes 196616 | tf_op jit(solution)/shard_map/ppermute | solution.py:34
  217.3 48.9 %collective-permute-start.41 = (bf16[32,1152]{1,0:T(8,128)(2,1)S(1)}, bf16[32,1152]{1,0:T(8,128)(2,1)S(1)}, u32[]{:S(2)}, u32[]{:S(2)}) collective-permute-start(bf16[32,1152]{1,0:T(8,128)(2,1)S(1)} %concatenate.133), channel_id=1, source_target_pairs={{0,24},{4,28},{8,0},{12,4},{16,8},{20,12},{24,16},{28,20},{1,25},{... | collective-permute-start | bytes 221192 | tf_op jit(solution)/shard_map/ppermute | solution.py:18
  218.7 18.5 %collective-permute-start.36 = (bf16[2,2,32,1024]{3,2,1,0:T(8,128)(2,1)S(1)}, bf16[2,2,32,1024]{3,2,1,0:T(8,128)(2,1)S(1)}, u32[]{:S(2)}, u32[]{:S(2)}) collective-permute-start(bf16[2,2,32,1024]{3,2,1,0:T(8,128)(2,1)S(1)} %slice_bitcast_fusion.2), channel_id=1, source_target_pairs={{0,1},{1,0},{2,3},{3,2},{4,5},{5,4},{6,7},{7,6},{8,9},{9,8},{10,11... | collective-permute-start | bytes 786440 | tf_op jit(solution)/shard_map/ppermute | solution.py:21
  219.3 10.3 %collective-permute-start.43 = (bf16[128,896]{1,0:T(8,128)(2,1)S(1)}, bf16[128,896]{1,0:T(8,128)(2,1)S(1)}, u32[]{:S(2)}, u32[]{:S(2)}) collective-permute-start(bf16[128,896]{1,0:T(8,128)(2,1)S(1)} %collective-permute-done.33), channel_id=1, source_target_pairs={{0,8},{4,12},{8,16},{12,20},{16,24},{20,28},{24,0},{28,4},{1,9},{5... | collective-permute-start | bytes 688136 | tf_op jit(solution)/shard_map/ppermute | solution.py:18
  219.4 14.0 %collective-permute-start.42 = (bf16[128,896]{1,0:T(8,128)(2,1)S(1)}, bf16[128,896]{1,0:T(8,128)(2,1)S(1)}, u32[]{:S(2)}, u32[]{:S(2)}) collective-permute-start(bf16[128,896]{1,0:T(8,128)(2,1)S(1)} %collective-permute-done.32), channel_id=1, source_target_pairs={{0,8},{4,12},{8,16},{12,20},{16,24},{20,28},{24,0},{28,4},{1,9},{5... | collective-permute-start | bytes 688136 | tf_op jit(solution)/shard_map/ppermute | solution.py:18
  237.3 5.8 %collective-permute-start.39 = (bf16[32,1024]{1,0:T(8,128)(2,1)S(1)}, bf16[32,1024]{1,0:T(8,128)(2,1)S(1)}, u32[]{:S(2)}, u32[]{:S(2)}) collective-permute-start(bf16[32,1024]{1,0:T(8,128)(2,1)S(1)} %get-tuple-element.63), channel_id=1, source_target_pairs={{0,6},{1,7},{2,4},{3,5},{4,2},{5,3},{6,0},{7,1},{8,14},{9,15},{10,... | collective-permute-start | bytes 196616 | tf_op jit(solution)/shard_map/ppermute | solution.py:34
  239.0 5.1 %collective-permute-start.38 = (bf16[32,1024]{1,0:T(8,128)(2,1)S(1)}, bf16[32,1024]{1,0:T(8,128)(2,1)S(1)}, u32[]{:S(2)}, u32[]{:S(2)}) collective-permute-start(bf16[32,1024]{1,0:T(8,128)(2,1)S(1)} %get-tuple-element.64), channel_id=1, source_target_pairs={{0,4},{1,5},{2,6},{3,7},{4,0},{5,1},{6,2},{7,3},{8,12},{9,13},{10,... | collective-permute-start | bytes 196616 | tf_op jit(solution)/shard_map/ppermute | solution.py:34
  239.5 4.6 %collective-permute-start.37 = (bf16[32,1024]{1,0:T(8,128)(2,1)S(1)}, bf16[32,1024]{1,0:T(8,128)(2,1)S(1)}, u32[]{:S(2)}, u32[]{:S(2)}) collective-permute-start(bf16[32,1024]{1,0:T(8,128)(2,1)S(1)} %get-tuple-element.62), channel_id=1, source_target_pairs={{0,2},{1,3},{2,0},{3,1},{4,6},{5,7},{6,4},{7,5},{8,10},{9,11},{10,... | collective-permute-start | bytes 196616 | tf_op jit(solution)/shard_map/ppermute | solution.py:34
  243.2 41.3 %collective-permute-start.58 = (bf16[896,512]{1,0:T(8,128)(2,1)S(1)}, bf16[896,512]{1,0:T(8,128)(2,1)S(1)}, u32[]{:S(2)}, u32[]{:S(2)}) collective-permute-start(bf16[896,512]{1,0:T(8,128)(2,1)S(1)} %get-tuple-element.31), channel_id=1, source_target_pairs={{0,4},{4,0},{8,12},{12,8},{16,20},{20,16},{24,28},{28,24},{1,5},{5... | collective-permute-start | bytes 2752520 | tf_op jit(solution)/shard_map/ppermute | solution.py:24
  244.1 1.5 collective-permute-start.46
  244.1 39.2 %copy-start.9 = (f32[4096]{0:T(1024)S(1)}, f32[4096]{0:T(1024)}, u32[]{:S(2)}) copy-start(f32[4096]{0:T(1024)} %param.15) | copy-start | bytes 49156
  245.7 5.8 %collective-permute-start.49 = (bf16[32,1024]{1,0:T(8,128)(2,1)S(1)}, bf16[32,1024]{1,0:T(8,128)(2,1)S(1)}, u32[]{:S(2)}, u32[]{:S(2)}) collective-permute-start(bf16[32,1024]{1,0:T(8,128)(2,1)S(1)} %get-tuple-element.56), channel_id=1, source_target_pairs={{0,6},{1,7},{2,4},{3,5},{4,2},{5,3},{6,0},{7,1},{8,14},{9,15},{10,... | collective-permute-start | bytes 196616 | tf_op jit(solution)/shard_map/ppermute | solution.py:34
  246.8 19.3 %collective-permute-start.48 = (bf16[32,1024]{1,0:T(8,128)(2,1)S(1)}, bf16[32,1024]{1,0:T(8,128)(2,1)S(1)}, u32[]{:S(2)}, u32[]{:S(2)}) collective-permute-start(bf16[32,1024]{1,0:T(8,128)(2,1)S(1)} %get-tuple-element.57), channel_id=1, source_target_pairs={{0,4},{1,5},{2,6},{3,7},{4,0},{5,1},{6,2},{7,3},{8,12},{9,13},{10,... | collective-permute-start | bytes 196616 | tf_op jit(solution)/shard_map/ppermute | solution.py:34
  248.0 18.1 %collective-permute-start.47 = (bf16[32,1024]{1,0:T(8,128)(2,1)S(1)}, bf16[32,1024]{1,0:T(8,128)(2,1)S(1)}, u32[]{:S(2)}, u32[]{:S(2)}) collective-permute-start(bf16[32,1024]{1,0:T(8,128)(2,1)S(1)} %get-tuple-element.55), channel_id=1, source_target_pairs={{0,2},{1,3},{2,0},{3,1},{4,6},{5,7},{6,4},{7,5},{8,10},{9,11},{10,... | collective-permute-start | bytes 196616 | tf_op jit(solution)/shard_map/ppermute | solution.py:34
  251.4 19.7 %collective-permute-start.30 = (bf16[32,1024]{1,0:T(8,128)(2,1)S(1)}, bf16[32,1024]{1,0:T(8,128)(2,1)S(1)}, u32[]{:S(2)}, u32[]{:S(2)}) collective-permute-start(bf16[32,1024]{1,0:T(8,128)(2,1)S(1)} %get-tuple-element.78), channel_id=1, source_target_pairs={{0,24},{4,28},{8,0},{12,4},{16,8},{20,12},{24,16},{28,20},{1,25},{... | collective-permute-start | bytes 196616 | tf_op jit(solution)/shard_map/ppermute | solution.py:18
  266.4 1.2 collective-permute-start.51
  267.7 4.5 %collective-permute-start.54 = (f32[1024]{0:T(1024)S(1)}, f32[1024]{0:T(1024)S(1)}, u32[]{:S(2)}, u32[]{:S(2)}) collective-permute-start(f32[1024]{0:T(1024)S(1)} %add.400), channel_id=1, source_target_pairs={{0,6},{1,7},{2,4},{3,5},{4,2},{5,3},{6,0},{7,1},{8,14},{9,15},{10,... | collective-permute-start | bytes 12296 | tf_op jit(solution)/shard_map/ppermute | solution.py:34
  269.0 3.6 %collective-permute-start.53 = (f32[1024]{0:T(1024)S(1)}, f32[1024]{0:T(1024)S(1)}, u32[]{:S(2)}, u32[]{:S(2)}) collective-permute-start(f32[1024]{0:T(1024)S(1)} %add.400), channel_id=1, source_target_pairs={{0,4},{1,5},{2,6},{3,7},{4,0},{5,1},{6,2},{7,3},{8,12},{9,13},{10,... | collective-permute-start | bytes 12296 | tf_op jit(solution)/shard_map/ppermute | solution.py:34
  269.6 3.6 %collective-permute-start.52 = (f32[1024]{0:T(1024)S(1)}, f32[1024]{0:T(1024)S(1)}, u32[]{:S(2)}, u32[]{:S(2)}) collective-permute-start(f32[1024]{0:T(1024)S(1)} %add.400), channel_id=1, source_target_pairs={{0,2},{1,3},{2,0},{3,1},{4,6},{5,7},{6,4},{7,5},{8,10},{9,11},{10,... | collective-permute-start | bytes 12296 | tf_op jit(solution)/shard_map/ppermute | solution.py:34
  271.2 5.2 %collective-permute-start.40 = (bf16[32,1024]{1,0:T(8,128)(2,1)S(1)}, bf16[32,1024]{1,0:T(8,128)(2,1)S(1)}, u32[]{:S(2)}, u32[]{:S(2)}) collective-permute-start(bf16[32,1024]{1,0:T(8,128)(2,1)S(1)} %get-tuple-element.80), channel_id=1, source_target_pairs={{0,16},{4,20},{8,24},{12,28},{16,0},{20,4},{24,8},{28,12},{1,17},{... | collective-permute-start | bytes 196616 | tf_op jit(solution)/shard_map/ppermute | solution.py:18
  273.2 7.6 %collective-permute-start.55 = (f32[1024]{0:T(1024)S(1)}, f32[1024]{0:T(1024)S(1)}, u32[]{:S(2)}, u32[]{:S(2)}) collective-permute-start(f32[1024]{0:T(1024)S(1)} %get-tuple-element.20), channel_id=1, source_target_pairs={{0,24},{4,28},{8,0},{12,4},{16,8},{20,12},{24,16},{28,20},{1,25},{... | collective-permute-start | bytes 12296 | tf_op jit(solution)/shard_map/ppermute | solution.py:18
  276.4 6.8 %collective-permute-start.50 = (bf16[32,1024]{1,0:T(8,128)(2,1)S(1)}, bf16[32,1024]{1,0:T(8,128)(2,1)S(1)}, u32[]{:S(2)}, u32[]{:S(2)}) collective-permute-start(bf16[32,1024]{1,0:T(8,128)(2,1)S(1)} %get-tuple-element.82), channel_id=1, source_target_pairs={{0,8},{4,12},{8,16},{12,20},{16,24},{20,28},{24,0},{28,4},{1,9},{5... | collective-permute-start | bytes 196616 | tf_op jit(solution)/shard_map/ppermute | solution.py:18
  276.4 4.6 %collective-permute-start.56 = (f32[1024]{0:T(1024)S(1)}, f32[1024]{0:T(1024)S(1)}, u32[]{:S(2)}, u32[]{:S(2)}) collective-permute-start(f32[1024]{0:T(1024)S(1)} %get-tuple-element.20), channel_id=1, source_target_pairs={{0,16},{4,20},{8,24},{12,28},{16,0},{20,4},{24,8},{28,12},{1,17},{... | collective-permute-start | bytes 12296 | tf_op jit(solution)/shard_map/ppermute | solution.py:18
  277.1 5.5 %collective-permute-start.57 = (f32[1024]{0:T(1024)S(1)}, f32[1024]{0:T(1024)S(1)}, u32[]{:S(2)}, u32[]{:S(2)}) collective-permute-start(f32[1024]{0:T(1024)S(1)} %get-tuple-element.20), channel_id=1, source_target_pairs={{0,8},{4,12},{8,16},{12,20},{16,24},{20,28},{24,0},{28,4},{1,9},{5... | collective-permute-start | bytes 12296 | tf_op jit(solution)/shard_map/ppermute | solution.py:18
  (8 other events, 12.2 us)
where the time goes:
time: 286 us
  waiting for transfers between devices  185 us (65%)
  starting transfers between devices  49.5 us (17%)
  matrix products  17.5 us (6%)
  other arithmetic  17.3 us (6%)
  local copies, waits for them, and re-layouts  14.6 us (5%)
    ppermute x30, waiting for transfers between devices, move_a(): return lax.ppermute(value, 'dp', ring(k % na))  116 us
    ppermute x18, waiting for transfers between devices, move_br(): return lax.ppermute(value, ('dp', 'tensor'), pairs)  64.1 us
    ppermute x30, starting transfers between devices, move_a(): return lax.ppermute(value, 'dp', ring(k % na))  22.6 us
    ppermute x18, starting transfers between devices, move_br(): return lax.ppermute(value, ('dp', 'tensor'), pairs)  21.7 us
    dot_general x4, matrix products, per_device(): jnp.einsum('grf,gdf->rd', jnp.stack((grad_gate, grad_up)), weight_pair, p...  12.7 us
  transfers between devices with their start and end apart: 59, of which 35 were waited for; matrix products, arithmetic and copies ran while one was open for 15% of the time, Pallas kernels for 0%

commit v1 on v0

--- a/solution.py
+++ b/solution.py
@@ -56,6 +56,11 @@
                 jnp.concatenate((given, kept), axis=axis),
             )
 
+        down_rows = down_weight.reshape(2, hidden, own)
+        down_keep = lax.dynamic_index_in_dim(down_rows, b, 0, False)
+        down_give = lax.dynamic_index_in_dim(down_rows, 1 - b, 0, False)
+        down_pair = ordered(down_keep, move_pair(down_give), 1)
+
         def halves(value):
             low, high = value[..., :hidden], value[..., hidden:]
             return jnp.where(first, low, high), jnp.where(first, high, low)
@@ -74,11 +79,6 @@
         up_keep, up_give = halves(relative_rows(up_pre))
         pre = [[jnp.stack((gate_keep, up_keep)), move_pair(jnp.stack((gate_give, up_give)))]]
 
-        down_rows = down_weight.reshape(2, hidden, own)
-        down_keep = lax.dynamic_index_in_dim(down_rows, b, 0, False)
-        down_give = lax.dynamic_index_in_dim(down_rows, 1 - b, 0, False)
-        down_pair = ordered(down_keep, move_pair(down_give), 1)
-
         inputs = tokens_in.astype(F32)
         inv_rms = lax.rsqrt(jnp.mean(inputs * inputs, axis=1, keepdims=True) + 1e-05)
         normed = inputs * inv_rms
@@ -93,23 +93,16 @@
         )
         every_out = []
         for kb in range(2):
-            mine = jnp.stack(
-                [near if kb == 0 and kr == 0 else move_br(near, kb, kr) for kr in range(nr)]
-            )
+            pieces = [near if kb == 0 and kr == 0 else move_br(near, kb, kr) for kr in range(nr)]
+            mine = jnp.stack(pieces)
             both = jnp.stack((mine, move_core(mine)))
             every_out.append(both.transpose(2, 1, 0, 3, 4).reshape(na, group, pair))
-
-        near_normed = []
-        for k in range(na):
-            message = jnp.concatenate((block_of(tokens_in, k), extra), axis=1)
-            if k:
-                message = move_a(message, k)
-            near_normed.append(message)
 
         gate_w_keep, gate_w_give = halves(gate_weight)
         up_w_keep, up_w_give = halves(up_weight)
         weight_keep = jnp.stack((gate_w_keep, up_w_keep))
-        weight_give = move_pair(jnp.stack((gate_w_give, up_w_give)))
+        weight_give = jnp.stack((gate_w_give, up_w_give))
+        weight_give = move_pair(weight_give)
         weight_pair = jnp.zeros((2, pair, hidden), BF16)
         weight_pair = lax.dynamic_update_slice_in_dim(weight_pair, weight_keep, b * own, 1)
         weight_pair = lax.dynamic_update_slice_in_dim(weight_pair, weight_give, (1 - b) * own, 1)
@@ -127,22 +120,30 @@
             ).astype(BF16).reshape(na, group, hidden)
             running = partial[1]
             for step in range(1, na):
-                running = (
-                    move_a(running, 1).astype(F32)
-                    + partial[(step + 1) % na].astype(F32)
-                ).astype(BF16)
+                theirs = move_a(running, 1)
+                running = (theirs.astype(F32) + partial[(step + 1) % na].astype(F32)).astype(BF16)
             grads[0][kb] = running
+        late_inputs, late_extra, grads[0][1] = lax.optimization_barrier(
+            (tokens_in, extra, grads[0][1])
+        )
+        near_normed = []
+        for k in range(na):
+            message = jnp.concatenate((block_of(late_inputs, k), late_extra), axis=1)
+            if k:
+                message = move_a(message, k)
+            near_normed.append(message)
+        for kb in range(2):
             for k in range(1, na):
                 grads[k][kb] = move_a(grads[k - 1][kb], 1)
 
+        pre_parts = [tuple(parts) for parts in pre]
         acts, norm_blocks = [], []
         gain_part = jnp.zeros((pair,), F32)
         for k in range(na):
-            value = jnp.concatenate(pre[k], axis=1).astype(F32)
+            value = jnp.concatenate(pre_parts[k], axis=1).astype(F32)
             gate_value, up_value = value[0], value[1]
             gate_sigmoid = jax.nn.sigmoid(gate_value)
             gate_silu = gate_value * gate_sigmoid
-            acts.append((gate_silu * up_value).astype(BF16))
             grad_act = jnp.concatenate(grads[k]).astype(F32)
             grad_gate = (
                 grad_act * up_value * gate_sigmoid * (1.0 + gate_value * (1.0 - gate_sigmoid))
@@ -164,15 +165,19 @@
                         piece = cores[kb, kr]
                         piece = move_br(piece, kb, -kr)
                         total = total + piece.astype(F32)
+            block = total.astype(BF16)
+            norm_blocks.append(move_a(block, -k) if k else block)
             message, total = lax.optimization_barrier((near_normed[k], total))
             tail = message[:, pair:].astype(F32)
             their_inputs = message[:, :pair]
             their_inv = tail[:, 0:1] + tail[:, 1:2] + tail[:, 2:3]
             their_normed = their_inputs.astype(F32) * their_inv
             gain_part = gain_part + jnp.sum(total * their_normed, axis=0)
-            total = total.astype(BF16)
-            norm_blocks.append(move_a(total, -k) if k else total)
-
+
+        for k in range(na):
+            value = jnp.concatenate(pre_parts[k], axis=1).astype(F32)
+            gate_value, up_value = value[0], value[1]
+            acts.append((gate_value * jax.nn.sigmoid(gate_value) * up_value).astype(BF16))
         down_both = lax.dot_general(
             jnp.concatenate(acts),
             jnp.concatenate(every_out, axis=1).reshape(na * 2 * group, pair),
@@ -201,7 +206,8 @@
         grad_norm = natural(norm_blocks, 1).astype(F32)
         scaled = grad_norm * norm_gain
         inner = jnp.mean(scaled * normed, axis=1, keepdims=True)
-        input_grad = (grad_out.astype(F32) + inv_rms * (scaled - normed * inner)).astype(BF16)
+        step = inv_rms * (scaled - normed * inner)
+        input_grad = (grad_out.astype(F32) + step).astype(BF16)
         return (input_grad, gain_grad, down_grad)
 
     return per_device

time: 286 us -> 276 us (0.965)
  waiting for transfers between devices: 185 us -> 170 us
    ppermute x30, waiting for transfers between devices: 116 us -> 98.3 us  [move_a(): return lax.ppermute(value, 'dp', ring(k % na))]
  transfers between devices with their start and end apart: 59 -> 59, of which waited for: 35 -> 34; matrix products, arithmetic and copies ran while one was open for 15% -> 17% of each run, Pallas kernels for 0% -> 0%
where the time goes in v1:
time: 276 us; the launch traced here: 275 us
  waiting for transfers between devices  170 us (62%)
  starting transfers between devices  51.5 us (19%)
  other arithmetic  19.6 us (7%)
  matrix products  17.4 us (6%)
  local copies, waits for them, and re-layouts  14.9 us (5%)
    ppermute x30, waiting for transfers between devices, move_a(): return lax.ppermute(value, 'dp', ring(k % na))  98.3 us
    ppermute x18, waiting for transfers between devices, move_br(): return lax.ppermute(value, ('dp', 'tensor'), pairs)  66.9 us
    ppermute x30, starting transfers between devices, move_a(): return lax.ppermute(value, 'dp', ring(k % na))  23.2 us
    ppermute x18, starting transfers between devices, move_br(): return lax.ppermute(value, ('dp', 'tensor'), pairs)  21.9 us
    dot_general x4, matrix products, per_device(): jnp.einsum('grf,gdf->rd', jnp.stack((grad_gate, grad_up)), weight_pair, p...  12.7 us
    ppermute x4, starting transfers between devices, move_pair(): return lax.ppermute(value, 'dp', [(d, d ^ 1) for d in range(groups)])  5.67 us
  transfers between devices with their start and end apart: 59, of which 34 were waited for; matrix products, arithmetic and copies ran while one was open for 17% of the time, Pallas kernels for 0%

profile of v1, /device:TPU:0, one launch (start us, length us, event | category | flops | bytes accessed | tf_op | source)
XLA Modules:
  0.0 275.2 jit_solution(4318663409516813396)
XLA Ops:
  0.6 2.3 select_bitcast_fusion
  3.0 1.4 pad_maximum_fusion.1
  4.4 3.0 %collective-permute-start.16 = (bf16[2,512,896]{2,1,0:T(8,128)(2,1)}, bf16[2,512,896]{2,1,0:T(8,128)(2,1)}, u32[]{:S(2)}, u32[]{:S(2)}) collective-permute-start(bf16[2,512,896]{2,1,0:T(8,128)(2,1)} %pad_maximum_fusion.1), channel_id=1, source_target_pairs={{0,4},{4,0},{8,12},{12,8},{16,20},{20,16},{24,28},{28,24},{1,5},{5... | collective-permute-start | bytes 5505032 | tf_op jit(solution)/shard_map/ppermute | solution.py:24
  9.2 3.6 %collective-permute-start.2 = (bf16[32,1024]{1,0:T(8,128)(2,1)}, bf16[32,1024]{1,0:T(8,128)(2,1)S(1)}, u32[]{:S(2)}, u32[]{:S(2)}) collective-permute-start(bf16[32,1024]{1,0:T(8,128)(2,1)} %get-tuple-element.89), channel_id=1, source_target_pairs={{0,24},{4,28},{8,0},{12,4},{16,8},{20,12},{24,16},{28,20},{1,25},{... | collective-permute-start | bytes 196616 | tf_op jit(solution)/shard_map/ppermute | solution.py:18
  18.1 2.8 %dynamic-slice_bitcast_fusion.1 = (bf16[896,512]{1,0:T(8,128)(2,1)}, bf16[896,512]{1,0:T(8,128)(2,1)}) fusion(bf16[2,896,512]{2,1,0:T(8,128)(2,1)} %bitcast.276, s32[]{:T(128)S(6)} %select_n.195, s32[]{:T(128)S(6)} %select_n.196), kind=kLoop, calls=%fused_computation.103 | loop fusion | bytes 3670024 | tf_op jit(solution)/shard_map/jit(dynamic_index_in_dim)/squeeze | solution.py:60
  21.6 1.7 fusion.94
  23.3 2.3 collective-permute-start.10
  26.8 2.1 broadcast_in_dim.13
  28.9 1.4 maximum_dynamic-update-slice_fusion
  30.3 3.4 %collective-permute-done.10 = bf16[4,32,1024]{2,1,0:T(8,128)(2,1)} collective-permute-done((bf16[4,32,1024]{2,1,0:T(8,128)(2,1)}, bf16[4,32,1024]{2,1,0:T(8,128)(2,1)}, u32[]{:S(2)}, u32[]{:S(2)}) %collective-permute-start.10) | collective-permute-done | bytes 262176 | tf_op jit(solution)/shard_map/ppermute | solution.py:34
  33.7 1.4 collective-permute-start.5
  35.1 34.6 %collective-permute-done.9 = bf16[4,32,1024]{2,1,0:T(8,128)(2,1)} collective-permute-done((bf16[4,32,1024]{2,1,0:T(8,128)(2,1)}, bf16[4,32,1024]{2,1,0:T(8,128)(2,1)}, u32[]{:S(2)}, u32[]{:S(2)}) %collective-permute-start.9) | collective-permute-done | bytes 262176 | tf_op jit(solution)/shard_map/ppermute | solution.py:34
  69.7 2.1 collective-permute-start.23
  71.7 1.1 fusion.92
  74.5 1.1 maximum_convert_fusion
  76.0 6.3 %collective-permute-done.23 = bf16[2,128,896]{2,1,0:T(8,128)(2,1)S(1)} collective-permute-done((bf16[2,128,896]{2,1,0:T(8,128)(2,1)S(1)}, bf16[2,128,896]{2,1,0:T(8,128)(2,1)S(1)}, u32[]{:S(2)}, u32[]{:S(2)}) %collective-permute-start.23) | collective-permute-done | bytes 458784 | tf_op jit(solution)/shard_map/ppermute | solution.py:18
  82.3 1.5 collective-permute-start.32
  84.3 4.1 %collective-permute-done.5 = bf16[896,512]{1,0:T(8,128)(2,1)S(1)} collective-permute-done((bf16[896,512]{1,0:T(8,128)(2,1)}, bf16[896,512]{1,0:T(8,128)(2,1)S(1)}, u32[]{:S(2)}, u32[]{:S(2)}) %collective-permute-start.5) | collective-permute-done | bytes 917536 | tf_op jit(solution)/shard_map/ppermute | solution.py:24
  88.4 1.3 convolution_convert_fusion
  89.7 1.9 collective-permute-start.12
  91.6 1.3 convolution_convert_fusion.1
  92.9 1.6 collective-permute-start.6
  94.5 3.2 %collective-permute-done.24 = bf16[2,128,896]{2,1,0:T(8,128)(2,1)S(1)} collective-permute-done((bf16[2,128,896]{2,1,0:T(8,128)(2,1)}, bf16[2,128,896]{2,1,0:T(8,128)(2,1)S(1)}, u32[]{:S(2)}, u32[]{:S(2)}) %collective-permute-start.24) | collective-permute-done | bytes 458784 | tf_op jit(solution)/shard_map/ppermute | solution.py:18
  97.8 9.7 %collective-permute-done.32 = bf16[2,128,896]{2,1,0:T(8,128)(2,1)S(1)} collective-permute-done((bf16[2,128,896]{2,1,0:T(8,128)(2,1)S(1)}, bf16[2,128,896]{2,1,0:T(8,128)(2,1)S(1)}, u32[]{:S(2)}, u32[]{:S(2)}) %collective-permute-start.32) | collective-permute-done | bytes 458784 | tf_op jit(solution)/shard_map/ppermute | solution.py:18
  107.8 4.6 %collective-permute-done.12 = bf16[128,896]{1,0:T(8,128)(2,1)S(1)} collective-permute-done((bf16[128,896]{1,0:T(8,128)(2,1)S(1)}, bf16[128,896]{1,0:T(8,128)(2,1)S(1)}, u32[]{:S(2)}, u32[]{:S(2)}) %collective-permute-start.12) | collective-permute-done | bytes 229408 | tf_op jit(solution)/shard_map/ppermute | solution.py:18
  112.6 4.8 %collective-permute-done.6 = bf16[128,896]{1,0:T(8,128)(2,1)S(1)} collective-permute-done((bf16[128,896]{1,0:T(8,128)(2,1)S(1)}, bf16[128,896]{1,0:T(8,128)(2,1)S(1)}, u32[]{:S(2)}, u32[]{:S(2)}) %collective-permute-start.6) | collective-permute-done | bytes 229408 | tf_op jit(solution)/shard_map/ppermute | solution.py:18
  117.5 24.5 %collective-permute-done.13 = bf16[128,896]{1,0:T(8,128)(2,1)S(1)} collective-permute-done((bf16[128,896]{1,0:T(8,128)(2,1)S(1)}, bf16[128,896]{1,0:T(8,128)(2,1)S(1)}, u32[]{:S(2)}, u32[]{:S(2)}) %collective-permute-start.13) | collective-permute-done | bytes 229408 | tf_op jit(solution)/shard_map/ppermute | solution.py:18
  142.1 4.8 %collective-permute-done.7 = bf16[128,896]{1,0:T(8,128)(2,1)S(1)} collective-permute-done((bf16[128,896]{1,0:T(8,128)(2,1)S(1)}, bf16[128,896]{1,0:T(8,128)(2,1)S(1)}, u32[]{:S(2)}, u32[]{:S(2)}) %collective-permute-start.7) | collective-permute-done | bytes 229408 | tf_op jit(solution)/shard_map/ppermute | solution.py:18
  147.5 5.0 %collective-permute-done.14 = bf16[128,896]{1,0:T(8,128)(2,1)S(1)} collective-permute-done((bf16[128,896]{1,0:T(8,128)(2,1)S(1)}, bf16[128,896]{1,0:T(8,128)(2,1)S(1)}, u32[]{:S(2)}, u32[]{:S(2)}) %collective-permute-start.14) | collective-permute-done | bytes 229408 | tf_op jit(solution)/shard_map/ppermute | solution.py:18
  152.6 4.9 %collective-permute-done.8 = bf16[128,896]{1,0:T(8,128)(2,1)S(1)} collective-permute-done((bf16[128,896]{1,0:T(8,128)(2,1)S(1)}, bf16[128,896]{1,0:T(8,128)(2,1)S(1)}, u32[]{:S(2)}, u32[]{:S(2)}) %collective-permute-start.8) | collective-permute-done | bytes 229408 | tf_op jit(solution)/shard_map/ppermute | solution.py:18
  158.2 4.0 %collective-permute-start.50 = (bf16[32,1152]{1,0:T(8,128)(2,1)S(1)}, bf16[32,1152]{1,0:T(8,128)(2,1)S(1)}, u32[]{:S(2)}, u32[]{:S(2)}) collective-permute-start(bf16[32,1152]{1,0:T(8,128)(2,1)S(1)} %get-tuple-element.93), channel_id=1, source_target_pairs={{0,24},{4,28},{8,0},{12,4},{16,8},{20,12},{24,16},{28,20},{1,25},{... | collective-permute-start | bytes 221192 | tf_op jit(solution)/shard_map/ppermute | solution.py:18
  162.3 2.9 %constant_dynamic-update-slice_fusion.15 = bf16[2,1024,896]{2,1,0:T(8,128)(2,1)} fusion(bf16[2,1024,896]{2,1,0:T(8,128)(2,1)} %maximum_dynamic-update-slice_fusion, bf16[2,512,896]{2,1,0:T(8,128)(2,1)} %collective-permute-done.16, s32[]{:T(128)S(6)} %select_n.217), kind=kLoop, calls=%fused_computation.236 | loop fusion | bytes 3670020 | tf_op jit(solution)/shard_map/dynamic_update_slice | solution.py:108
  165.1 3.2 %fusion.11 = bf16[256,1024]{1,0:T(8,128)(2,1)S(1)} fusion(bf16[2,1024,896]{2,1,0:T(8,128)(2,1)} %constant_dynamic-update-slice_fusion.15, bf16[1,256,896]{2,1,0:T(8,128)(2,1)S(1)} %get-tuple-element.44, bf16[1,256,896]{2,1,0:T(8,128)(2,1)S(1)} %get-tuple-element.43), kind=kOutput, calls=%fused_computation.19 | convolution fusion | flops 940244992 | bytes 5111808 | tf_op jit(solution)/shard_map/grf,gdf->rd/dot_general | solution.py:152
  168.9 2.9 %collective-permute-done.22 = bf16[128,896]{1,0:T(8,128)(2,1)S(1)} collective-permute-done((bf16[128,896]{1,0:T(8,128)(2,1)S(1)}, bf16[128,896]{1,0:T(8,128)(2,1)S(1)}, u32[]{:S(2)}, u32[]{:S(2)}) %collective-permute-start.22) | collective-permute-done | bytes 229408 | tf_op jit(solution)/shard_map/ppermute | solution.py:18
  171.9 2.5 collective-permute-done.21
  174.9 3.2 %fusion.12 = bf16[256,1024]{1,0:T(8,128)(2,1)S(1)} fusion(bf16[2,1024,896]{2,1,0:T(8,128)(2,1)} %constant_dynamic-update-slice_fusion.15, bf16[1,256,896]{2,1,0:T(8,128)(2,1)S(1)} %get-tuple-element.42, bf16[1,256,896]{2,1,0:T(8,128)(2,1)S(1)} %get-tuple-element.41), kind=kOutput, calls=%fused_computation.20 | convolution fusion | flops 940244992 | bytes 5111808 | tf_op jit(solution)/shard_map/grf,gdf->rd/dot_general | solution.py:152
  178.1 2.1 fusion.8
  180.3 1.7 collective-permute-start.30
  182.0 6.1 %collective-permute-done.31 = bf16[128,896]{1,0:T(8,128)(2,1)S(1)} collective-permute-done((bf16[128,896]{1,0:T(8,128)(2,1)S(1)}, bf16[128,896]{1,0:T(8,128)(2,1)S(1)}, u32[]{:S(2)}, u32[]{:S(2)}) %collective-permute-start.31) | collective-permute-done | bytes 229408 | tf_op jit(solution)/shard_map/ppermute | solution.py:18
  188.1 2.5 collective-permute-done.30
  191.2 3.2 %fusion.13 = bf16[256,1024]{1,0:T(8,128)(2,1)S(1)} fusion(bf16[2,1024,896]{2,1,0:T(8,128)(2,1)} %constant_dynamic-update-slice_fusion.15, bf16[1,256,896]{2,1,0:T(8,128)(2,1)S(1)} %get-tuple-element.40, bf16[1,256,896]{2,1,0:T(8,128)(2,1)S(1)} %get-tuple-element.39), kind=kOutput, calls=%fused_computation.21 | convolution fusion | flops 940244992 | bytes 5111808 | tf_op jit(solution)/shard_map/grf,gdf->rd/dot_general | solution.py:152
  194.5 2.3 collective-permute-start.20
  198.1 1.6 collective-permute-done.20
  199.7 2.3 collective-permute-start.28
  202.6 1.4 collective-permute-start.26
  204.9 1.4 collective-permute-done.27
  207.1 3.9 %collective-permute-done.48 = bf16[32,1152]{1,0:T(8,128)(2,1)S(1)} collective-permute-done((bf16[32,1152]{1,0:T(8,128)(2,1)S(1)}, bf16[32,1152]{1,0:T(8,128)(2,1)S(1)}, u32[]{:S(2)}, u32[]{:S(2)}) %collective-permute-start.48) | collective-permute-done | bytes 73760 | tf_op jit(solution)/shard_map/ppermute | solution.py:18
  211.4 5.8 %collective-permute-done.40 = bf16[128,896]{1,0:T(8,128)(2,1)S(1)} collective-permute-done((bf16[128,896]{1,0:T(8,128)(2,1)S(1)}, bf16[128,896]{1,0:T(8,128)(2,1)S(1)}, u32[]{:S(2)}, u32[]{:S(2)}) %collective-permute-start.40) | collective-permute-done | bytes 229408 | tf_op jit(solution)/shard_map/ppermute | solution.py:18
  217.2 3.8 %collective-permute-done.39 = bf16[128,896]{1,0:T(8,128)(2,1)S(1)} collective-permute-done((bf16[128,896]{1,0:T(8,128)(2,1)S(1)}, bf16[128,896]{1,0:T(8,128)(2,1)S(1)}, u32[]{:S(2)}, u32[]{:S(2)}) %collective-permute-start.39) | collective-permute-done | bytes 229408 | tf_op jit(solution)/shard_map/ppermute | solution.py:18
  221.6 3.2 %fusion.14 = bf16[256,1024]{1,0:T(8,128)(2,1)S(1)} fusion(bf16[2,1024,896]{2,1,0:T(8,128)(2,1)} %constant_dynamic-update-slice_fusion.15, bf16[1,256,896]{2,1,0:T(8,128)(2,1)S(1)} %get-tuple-element.38, bf16[1,256,896]{2,1,0:T(8,128)(2,1)S(1)} %get-tuple-element.37), kind=kOutput, calls=%fused_computation.22 | convolution fusion | flops 940244992 | bytes 5111808 | tf_op jit(solution)/shard_map/grf,gdf->rd/dot_general | solution.py:152
  224.9 2.2 collective-permute-start.37
  228.5 2.1 collective-permute-done.37
  233.0 1.9 collective-permute-start.46
  236.7 1.6 collective-permute-done.46
  238.2 1.3 collective-permute-done.45
  241.1 1.2 collective-permute-start.58
  242.3 1.1 collective-permute-start.54
  243.4 1.3 collective-permute-start.53
  246.9 17.1 %collective-permute-done.53 = f32[1024]{0:T(1024)S(1)} collective-permute-done((f32[1024]{0:T(1024)S(1)}, f32[1024]{0:T(1024)S(1)}, u32[]{:S(2)}, u32[]{:S(2)}) %collective-permute-start.53) | collective-permute-done | bytes 4128 | tf_op jit(solution)/shard_map/ppermute | solution.py:34
  264.5 1.7 collective-permute-start.47
  266.6 2.3 collective-permute-start.57
  268.9 1.8 collective-permute-done.56
  270.7 1.3 collective-permute-done.57
  274.0 1.2 copy-done.1
  (189 shorter events, 32.1 us)
Async XLA Ops:
  3.0 4.4 %copy-start.4 = (bf16[128,1792]{1,0:T(8,128)(2,1)S(1)}, bf16[128,1792]{1,0:T(8,128)(2,1)}, u32[]{:S(2)}) copy-start(bf16[128,1792]{1,0:T(8,128)(2,1)} %param.11) | copy-start | bytes 1376260
  3.0 4.5 %copy-start.5 = (bf16[128,1792]{1,0:T(8,128)(2,1)S(1)}, bf16[128,1792]{1,0:T(8,128)(2,1)}, u32[]{:S(2)}) copy-start(bf16[128,1792]{1,0:T(8,128)(2,1)} %param.10) | copy-start | bytes 1376260
  4.4 153.8 %collective-permute-start.16 = (bf16[2,512,896]{2,1,0:T(8,128)(2,1)}, bf16[2,512,896]{2,1,0:T(8,128)(2,1)}, u32[]{:S(2)}, u32[]{:S(2)}) collective-permute-start(bf16[2,512,896]{2,1,0:T(8,128)(2,1)} %pad_maximum_fusion.1), channel_id=1, source_target_pairs={{0,4},{4,0},{8,12},{12,8},{16,20},{20,16},{24,28},{28,24},{1,5},{5... | collective-permute-start | bytes 5505032 | tf_op jit(solution)/shard_map/ppermute | solution.py:24
  7.6 6.2 %copy-start = (bf16[32,4096]{1,0:T(8,128)(2,1)S(1)}, bf16[32,4096]{1,0:T(8,128)(2,1)}, u32[]{:S(2)}) copy-start(bf16[32,4096]{1,0:T(8,128)(2,1)} %param.8) | copy-start | bytes 786436
  7.8 66.2 %collective-permute-start.15 = (bf16[2,128,896]{2,1,0:T(8,128)(2,1)S(1)}, bf16[2,128,896]{2,1,0:T(8,128)(2,1)}, u32[]{:S(2)}, u32[]{:S(2)}) collective-permute-start(bf16[2,128,896]{2,1,0:T(8,128)(2,1)S(1)} %pad_maximum_fusion.9), channel_id=1, source_target_pairs={{0,4},{4,0},{8,12},{12,8},{16,20},{20,16},{24,28},{28,24},{1,5},{5... | collective-permute-start | bytes 1376264 | tf_op jit(solution)/shard_map/ppermute | solution.py:24
  9.2 11.8 %collective-permute-start.2 = (bf16[32,1024]{1,0:T(8,128)(2,1)}, bf16[32,1024]{1,0:T(8,128)(2,1)S(1)}, u32[]{:S(2)}, u32[]{:S(2)}) collective-permute-start(bf16[32,1024]{1,0:T(8,128)(2,1)} %get-tuple-element.89), channel_id=1, source_target_pairs={{0,24},{4,28},{8,0},{12,4},{16,8},{20,12},{24,16},{28,20},{1,25},{... | collective-permute-start | bytes 196616 | tf_op jit(solution)/shard_map/ppermute | solution.py:18
  12.8 8.2 %collective-permute-start.1 = (bf16[32,1024]{1,0:T(8,128)(2,1)}, bf16[32,1024]{1,0:T(8,128)(2,1)S(1)}, u32[]{:S(2)}, u32[]{:S(2)}) collective-permute-start(bf16[32,1024]{1,0:T(8,128)(2,1)} %get-tuple-element.90), channel_id=1, source_target_pairs={{0,16},{4,20},{8,24},{12,28},{16,0},{20,4},{24,8},{28,12},{1,17},{... | collective-permute-start | bytes 196616 | tf_op jit(solution)/shard_map/ppermute | solution.py:18
  12.8 8.2 %collective-permute-start = (bf16[32,1024]{1,0:T(8,128)(2,1)S(1)}, bf16[32,1024]{1,0:T(8,128)(2,1)S(1)}, u32[]{:S(2)}, u32[]{:S(2)}) collective-permute-start(bf16[32,1024]{1,0:T(8,128)(2,1)S(1)} %get-tuple-element.88), channel_id=1, source_target_pairs={{0,8},{4,12},{8,16},{12,20},{16,24},{20,28},{24,0},{28,4},{1,9},{5... | collective-permute-start | bytes 196616 | tf_op jit(solution)/shard_map/ppermute | solution.py:18
  23.3 10.4 %collective-permute-start.10 = (bf16[4,32,1024]{2,1,0:T(8,128)(2,1)}, bf16[4,32,1024]{2,1,0:T(8,128)(2,1)}, u32[]{:S(2)}, u32[]{:S(2)}) collective-permute-start(bf16[4,32,1024]{2,1,0:T(8,128)(2,1)} %get-tuple-element.86), channel_id=1, source_target_pairs={{0,6},{1,7},{2,4},{3,5},{4,2},{5,3},{6,0},{7,1},{8,14},{9,15},{10,... | collective-permute-start | bytes 786440 | tf_op jit(solution)/shard_map/ppermute | solution.py:34
  25.6 44.1 %collective-permute-start.9 = (bf16[4,32,1024]{2,1,0:T(8,128)(2,1)}, bf16[4,32,1024]{2,1,0:T(8,128)(2,1)}, u32[]{:S(2)}, u32[]{:S(2)}) collective-permute-start(bf16[4,32,1024]{2,1,0:T(8,128)(2,1)} %get-tuple-element.86), channel_id=1, source_target_pairs={{0,4},{1,5},{2,6},{3,7},{4,0},{5,1},{6,2},{7,3},{8,12},{9,13},{10,... | collective-permute-start | bytes 786440 | tf_op jit(solution)/shard_map/ppermute | solution.py:34
  26.3 46.6 %collective-permute-start.3 = (bf16[4,32,1024]{2,1,0:T(8,128)(2,1)}, bf16[4,32,1024]{2,1,0:T(8,128)(2,1)}, u32[]{:S(2)}, u32[]{:S(2)}) collective-permute-start(bf16[4,32,1024]{2,1,0:T(8,128)(2,1)} %get-tuple-element.86), channel_id=1, source_target_pairs={{0,2},{1,3},{2,0},{3,1},{4,6},{5,7},{6,4},{7,5},{8,10},{9,11},{10,... | collective-permute-start | bytes 786440 | tf_op jit(solution)/shard_map/ppermute | solution.py:34
  33.7 54.7 %collective-permute-start.5 = (bf16[896,512]{1,0:T(8,128)(2,1)}, bf16[896,512]{1,0:T(8,128)(2,1)S(1)}, u32[]{:S(2)}, u32[]{:S(2)}) collective-permute-start(bf16[896,512]{1,0:T(8,128)(2,1)} %get-tuple-element.48), channel_id=1, source_target_pairs={{0,4},{4,0},{8,12},{12,8},{16,20},{20,16},{24,28},{28,24},{1,5},{5... | collective-permute-start | bytes 2752520 | tf_op jit(solution)/shard_map/ppermute | solution.py:24
  69.7 12.6 %collective-permute-start.23 = (bf16[2,128,896]{2,1,0:T(8,128)(2,1)S(1)}, bf16[2,128,896]{2,1,0:T(8,128)(2,1)S(1)}, u32[]{:S(2)}, u32[]{:S(2)}) collective-permute-start(bf16[2,128,896]{2,1,0:T(8,128)(2,1)S(1)} %pad_maximum_fusion.8), channel_id=1, source_target_pairs={{0,8},{4,12},{8,16},{12,20},{16,24},{20,28},{24,0},{28,4},{1,9},{5... | collective-permute-start | bytes 1376264 | tf_op jit(solution)/shard_map/ppermute | solution.py:18
  72.9 9.5 %collective-permute-start.11 = (bf16[2,4,32,1024]{3,2,1,0:T(8,128)(2,1)S(1)}, bf16[2,4,32,1024]{3,2,1,0:T(8,128)(2,1)S(1)}, u32[]{:S(2)}, u32[]{:S(2)}) collective-permute-start(bf16[2,4,32,1024]{3,2,1,0:T(8,128)(2,1)S(1)} %get-tuple-element.56), channel_id=1, source_target_pairs={{0,1},{1,0},{2,3},{3,2},{4,5},{5,4},{6,7},{7,6},{8,9},{9,8},{10,11... | collective-permute-start | bytes 1572872 | tf_op jit(solution)/shard_map/ppermute | solution.py:21
  74.0 10.0 %collective-permute-start.4 = (bf16[2,4,32,1024]{3,2,0,1:T(8,128)(2,1)S(1)}, bf16[2,4,32,1024]{3,2,0,1:T(8,128)(2,1)S(1)}, u32[]{:S(2)}, u32[]{:S(2)}) collective-permute-start(bf16[2,4,32,1024]{3,2,0,1:T(8,128)(2,1)S(1)} %get-tuple-element.54), channel_id=1, source_target_pairs={{0,1},{1,0},{2,3},{3,2},{4,5},{5,4},{6,7},{7,6},{8,9},{9,8},{10,11... | collective-permute-start | bytes 1572872 | tf_op jit(solution)/shard_map/ppermute | solution.py:21
  82.3 15.4 %collective-permute-start.24 = (bf16[2,128,896]{2,1,0:T(8,128)(2,1)}, bf16[2,128,896]{2,1,0:T(8,128)(2,1)S(1)}, u32[]{:S(2)}, u32[]{:S(2)}) collective-permute-start(bf16[2,128,896]{2,1,0:T(8,128)(2,1)} %collective-permute-done.15), channel_id=1, source_target_pairs={{0,8},{4,12},{8,16},{12,20},{16,24},{20,28},{24,0},{28,4},{1,9},{5... | collective-permute-start | bytes 1376264 | tf_op jit(solution)/shard_map/ppermute | solution.py:18
  82.3 25.2 %collective-permute-start.32 = (bf16[2,128,896]{2,1,0:T(8,128)(2,1)S(1)}, bf16[2,128,896]{2,1,0:T(8,128)(2,1)S(1)}, u32[]{:S(2)}, u32[]{:S(2)}) collective-permute-start(bf16[2,128,896]{2,1,0:T(8,128)(2,1)S(1)} %collective-permute-done.23), channel_id=1, source_target_pairs={{0,8},{4,12},{8,16},{12,20},{16,24},{20,28},{24,0},{28,4},{1,9},{5... | collective-permute-start | bytes 1376264 | tf_op jit(solution)/shard_map/ppermute | solution.py:18
  89.7 22.7 %collective-permute-start.12 = (bf16[128,896]{1,0:T(8,128)(2,1)S(1)}, bf16[128,896]{1,0:T(8,128)(2,1)S(1)}, u32[]{:S(2)}, u32[]{:S(2)}) collective-permute-start(bf16[128,896]{1,0:T(8,128)(2,1)S(1)} %slice.300), channel_id=1, source_target_pairs={{0,8},{4,12},{8,16},{12,20},{16,24},{20,28},{24,0},{28,4},{1,9},{5... | collective-permute-start | bytes 688136 | tf_op jit(solution)/shard_map/ppermute | solution.py:18
  92.9 24.5 %collective-permute-start.6 = (bf16[128,896]{1,0:T(8,128)(2,1)S(1)}, bf16[128,896]{1,0:T(8,128)(2,1)S(1)}, u32[]{:S(2)}, u32[]{:S(2)}) collective-permute-start(bf16[128,896]{1,0:T(8,128)(2,1)S(1)} %slice.296), channel_id=1, source_target_pairs={{0,8},{4,12},{8,16},{12,20},{16,24},{20,28},{24,0},{28,4},{1,9},{5... | collective-permute-start | bytes 688136 | tf_op jit(solution)/shard_map/ppermute | solution.py:18
  97.7 49.3 %collective-permute-start.33 = (bf16[2,128,896]{2,1,0:T(8,128)(2,1)S(1)}, bf16[2,128,896]{2,1,0:T(8,128)(2,1)S(1)}, u32[]{:S(2)}, u32[]{:S(2)}) collective-permute-start(bf16[2,128,896]{2,1,0:T(8,128)(2,1)S(1)} %collective-permute-done.24), channel_id=1, source_target_pairs={{0,8},{4,12},{8,16},{12,20},{16,24},{20,28},{24,0},{28,4},{1,9},{5... | collective-permute-start | bytes 1376264 | tf_op jit(solution)/shard_map/ppermute | solution.py:18
  107.5 60.8 %collective-permute-start.41 = (bf16[2,128,896]{2,1,0:T(8,128)(2,1)S(1)}, bf16[2,128,896]{2,1,0:T(8,128)(2,1)S(1)}, u32[]{:S(2)}, u32[]{:S(2)}) collective-permute-start(bf16[2,128,896]{2,1,0:T(8,128)(2,1)S(1)} %collective-permute-done.32), channel_id=1, source_target_pairs={{0,8},{4,12},{8,16},{12,20},{16,24},{20,28},{24,0},{28,4},{1,9},{5... | collective-permute-start | bytes 1376264 | tf_op jit(solution)/shard_map/ppermute | solution.py:18
  112.5 29.4 %collective-permute-start.13 = (bf16[128,896]{1,0:T(8,128)(2,1)S(1)}, bf16[128,896]{1,0:T(8,128)(2,1)S(1)}, u32[]{:S(2)}, u32[]{:S(2)}) collective-permute-start(bf16[128,896]{1,0:T(8,128)(2,1)S(1)} %add_convert_fusion.2), channel_id=1, source_target_pairs={{0,8},{4,12},{8,16},{12,20},{16,24},{20,28},{24,0},{28,4},{1,9},{5... | collective-permute-start | bytes 688136 | tf_op jit(solution)/shard_map/ppermute | solution.py:18
  117.4 29.4 %collective-permute-start.7 = (bf16[128,896]{1,0:T(8,128)(2,1)S(1)}, bf16[128,896]{1,0:T(8,128)(2,1)S(1)}, u32[]{:S(2)}, u32[]{:S(2)}) collective-permute-start(bf16[128,896]{1,0:T(8,128)(2,1)S(1)} %add_convert_fusion.5), channel_id=1, source_target_pairs={{0,8},{4,12},{8,16},{12,20},{16,24},{20,28},{24,0},{28,4},{1,9},{5... | collective-permute-start | bytes 688136 | tf_op jit(solution)/shard_map/ppermute | solution.py:18
  142.0 10.4 %collective-permute-start.14 = (bf16[128,896]{1,0:T(8,128)(2,1)S(1)}, bf16[128,896]{1,0:T(8,128)(2,1)S(1)}, u32[]{:S(2)}, u32[]{:S(2)}) collective-permute-start(bf16[128,896]{1,0:T(8,128)(2,1)S(1)} %add_convert_fusion.1), channel_id=1, source_target_pairs={{0,8},{4,12},{8,16},{12,20},{16,24},{20,28},{24,0},{28,4},{1,9},{5... | collective-permute-start | bytes 688136 | tf_op jit(solution)/shard_map/ppermute | solution.py:18
  146.9 10.5 %collective-permute-start.8 = (bf16[128,896]{1,0:T(8,128)(2,1)S(1)}, bf16[128,896]{1,0:T(8,128)(2,1)S(1)}, u32[]{:S(2)}, u32[]{:S(2)}) collective-permute-start(bf16[128,896]{1,0:T(8,128)(2,1)S(1)} %add_convert_fusion.4), channel_id=1, source_target_pairs={{0,8},{4,12},{8,16},{12,20},{16,24},{20,28},{24,0},{28,4},{1,9},{5... | collective-permute-start | bytes 688136 | tf_op jit(solution)/shard_map/ppermute | solution.py:18
  147.0 21.4 %collective-permute-start.42 = (bf16[2,128,896]{2,1,0:T(8,128)(2,1)S(1)}, bf16[2,128,896]{2,1,0:T(8,128)(2,1)S(1)}, u32[]{:S(2)}, u32[]{:S(2)}) collective-permute-start(bf16[2,128,896]{2,1,0:T(8,128)(2,1)S(1)} %collective-permute-done.33), channel_id=1, source_target_pairs={{0,8},{4,12},{8,16},{12,20},{16,24},{20,28},{24,0},{28,4},{1,9},{5... | collective-permute-start | bytes 1376264 | tf_op jit(solution)/shard_map/ppermute | solution.py:18
  152.5 19.4 %collective-permute-start.22 = (bf16[128,896]{1,0:T(8,128)(2,1)S(1)}, bf16[128,896]{1,0:T(8,128)(2,1)S(1)}, u32[]{:S(2)}, u32[]{:S(2)}) collective-permute-start(bf16[128,896]{1,0:T(8,128)(2,1)S(1)} %add_convert_fusion), channel_id=1, source_target_pairs={{0,8},{4,12},{8,16},{12,20},{16,24},{20,28},{24,0},{28,4},{1,9},{5... | collective-permute-start | bytes 688136 | tf_op jit(solution)/shard_map/ppermute | solution.py:18
  157.5 16.8 %collective-permute-start.21 = (bf16[128,896]{1,0:T(8,128)(2,1)S(1)}, bf16[128,896]{1,0:T(8,128)(2,1)S(1)}, u32[]{:S(2)}, u32[]{:S(2)}) collective-permute-start(bf16[128,896]{1,0:T(8,128)(2,1)S(1)} %add_convert_fusion.3), channel_id=1, source_target_pairs={{0,8},{4,12},{8,16},{12,20},{16,24},{20,28},{24,0},{28,4},{1,9},{5... | collective-permute-start | bytes 688136 | tf_op jit(solution)/shard_map/ppermute | solution.py:18
  158.2 81.8 %collective-permute-start.50 = (bf16[32,1152]{1,0:T(8,128)(2,1)S(1)}, bf16[32,1152]{1,0:T(8,128)(2,1)S(1)}, u32[]{:S(2)}, u32[]{:S(2)}) collective-permute-start(bf16[32,1152]{1,0:T(8,128)(2,1)S(1)} %get-tuple-element.93), channel_id=1, source_target_pairs={{0,24},{4,28},{8,0},{12,4},{16,8},{20,12},{24,16},{28,20},{1,25},{... | collective-permute-start | bytes 221192 | tf_op jit(solution)/shard_map/ppermute | solution.py:18
  168.3 63.5 %collective-permute-start.49 = (bf16[32,1152]{1,0:T(8,128)(2,1)S(1)}, bf16[32,1152]{1,0:T(8,128)(2,1)S(1)}, u32[]{:S(2)}, u32[]{:S(2)}) collective-permute-start(bf16[32,1152]{1,0:T(8,128)(2,1)S(1)} %get-tuple-element.92), channel_id=1, source_target_pairs={{0,16},{4,20},{8,24},{12,28},{16,0},{20,4},{24,8},{28,12},{1,17},{... | collective-permute-start | bytes 221192 | tf_op jit(solution)/shard_map/ppermute | solution.py:18
  168.4 25.9 %collective-permute-start.17 = (bf16[2,2,32,1024]{3,2,1,0:T(8,128)(2,1)S(1)}, bf16[2,2,32,1024]{3,2,1,0:T(8,128)(2,1)S(1)}, u32[]{:S(2)}, u32[]{:S(2)}) collective-permute-start(bf16[2,2,32,1024]{3,2,1,0:T(8,128)(2,1)S(1)} %slice_bitcast_fusion.6), channel_id=1, source_target_pairs={{0,1},{1,0},{2,3},{3,2},{4,5},{5,4},{6,7},{7,6},{8,9},{9,8},{10,11... | collective-permute-start | bytes 786440 | tf_op jit(solution)/shard_map/ppermute | solution.py:21
  180.2 7.9 %collective-permute-start.31 = (bf16[128,896]{1,0:T(8,128)(2,1)S(1)}, bf16[128,896]{1,0:T(8,128)(2,1)S(1)}, u32[]{:S(2)}, u32[]{:S(2)}) collective-permute-start(bf16[128,896]{1,0:T(8,128)(2,1)S(1)} %collective-permute-done.22), channel_id=1, source_target_pairs={{0,8},{4,12},{8,16},{12,20},{16,24},{20,28},{24,0},{28,4},{1,9},{5... | collective-permute-start | bytes 688136 | tf_op jit(solution)/shard_map/ppermute | solution.py:18
  180.3 10.3 %collective-permute-start.30 = (bf16[128,896]{1,0:T(8,128)(2,1)S(1)}, bf16[128,896]{1,0:T(8,128)(2,1)S(1)}, u32[]{:S(2)}, u32[]{:S(2)}) collective-permute-start(bf16[128,896]{1,0:T(8,128)(2,1)S(1)} %collective-permute-done.21), channel_id=1, source_target_pairs={{0,8},{4,12},{8,16},{12,20},{16,24},{20,28},{24,0},{28,4},{1,9},{5... | collective-permute-start | bytes 688136 | tf_op jit(solution)/shard_map/ppermute | solution.py:18
  188.1 9.1 %collective-permute-start.25 = (bf16[2,2,32,1024]{3,2,1,0:T(8,128)(2,1)S(1)}, bf16[2,2,32,1024]{3,2,1,0:T(8,128)(2,1)S(1)}, u32[]{:S(2)}, u32[]{:S(2)}) collective-permute-start(bf16[2,2,32,1024]{3,2,1,0:T(8,128)(2,1)S(1)} %slice_bitcast_fusion.4), channel_id=1, source_target_pairs={{0,1},{1,0},{2,3},{3,2},{4,5},{5,4},{6,7},{7,6},{8,9},{9,8},{10,11... | collective-permute-start | bytes 786440 | tf_op jit(solution)/shard_map/ppermute | solution.py:21
  194.5 5.2 %collective-permute-start.20 = (bf16[32,1024]{1,0:T(8,128)(2,1)S(1)}, bf16[32,1024]{1,0:T(8,128)(2,1)S(1)}, u32[]{:S(2)}, u32[]{:S(2)}) collective-permute-start(bf16[32,1024]{1,0:T(8,128)(2,1)S(1)} %get-tuple-element.83), channel_id=1, source_target_pairs={{0,6},{1,7},{2,4},{3,5},{4,2},{5,3},{6,0},{7,1},{8,14},{9,15},{10,... | collective-permute-start | bytes 196616 | tf_op jit(solution)/shard_map/ppermute | solution.py:34
  196.7 5.3 %collective-permute-start.19 = (bf16[32,1024]{1,0:T(8,128)(2,1)S(1)}, bf16[32,1024]{1,0:T(8,128)(2,1)S(1)}, u32[]{:S(2)}, u32[]{:S(2)}) collective-permute-start(bf16[32,1024]{1,0:T(8,128)(2,1)S(1)} %get-tuple-element.84), channel_id=1, source_target_pairs={{0,4},{1,5},{2,6},{3,7},{4,0},{5,1},{6,2},{7,3},{8,12},{9,13},{10,... | collective-permute-start | bytes 196616 | tf_op jit(solution)/shard_map/ppermute | solution.py:34
  197.3 5.4 %collective-permute-start.18 = (bf16[32,1024]{1,0:T(8,128)(2,1)S(1)}, bf16[32,1024]{1,0:T(8,128)(2,1)S(1)}, u32[]{:S(2)}, u32[]{:S(2)}) collective-permute-start(bf16[32,1024]{1,0:T(8,128)(2,1)S(1)} %get-tuple-element.82), channel_id=1, source_target_pairs={{0,2},{1,3},{2,0},{3,1},{4,6},{5,7},{6,4},{7,5},{8,10},{9,11},{10,... | collective-permute-start | bytes 196616 | tf_op jit(solution)/shard_map/ppermute | solution.py:34
  199.7 5.2 %collective-permute-start.28 = (bf16[32,1024]{1,0:T(8,128)(2,1)S(1)}, bf16[32,1024]{1,0:T(8,128)(2,1)S(1)}, u32[]{:S(2)}, u32[]{:S(2)}) collective-permute-start(bf16[32,1024]{1,0:T(8,128)(2,1)S(1)} %get-tuple-element.80), channel_id=1, source_target_pairs={{0,6},{1,7},{2,4},{3,5},{4,2},{5,3},{6,0},{7,1},{8,14},{9,15},{10,... | collective-permute-start | bytes 196616 | tf_op jit(solution)/shard_map/ppermute | solution.py:34
  202.0 4.3 %collective-permute-start.27 = (bf16[32,1024]{1,0:T(8,128)(2,1)S(1)}, bf16[32,1024]{1,0:T(8,128)(2,1)S(1)}, u32[]{:S(2)}, u32[]{:S(2)}) collective-permute-start(bf16[32,1024]{1,0:T(8,128)(2,1)S(1)} %get-tuple-element.81), channel_id=1, source_target_pairs={{0,4},{1,5},{2,6},{3,7},{4,0},{5,1},{6,2},{7,3},{8,12},{9,13},{10,... | collective-permute-start | bytes 196616 | tf_op jit(solution)/shard_map/ppermute | solution.py:34
  202.6 4.3 %collective-permute-start.26 = (bf16[32,1024]{1,0:T(8,128)(2,1)S(1)}, bf16[32,1024]{1,0:T(8,128)(2,1)S(1)}, u32[]{:S(2)}, u32[]{:S(2)}) collective-permute-start(bf16[32,1024]{1,0:T(8,128)(2,1)S(1)} %get-tuple-element.79), channel_id=1, source_target_pairs={{0,2},{1,3},{2,0},{3,1},{4,6},{5,7},{6,4},{7,5},{8,10},{9,11},{10,... | collective-permute-start | bytes 196616 | tf_op jit(solution)/shard_map/ppermute | solution.py:34
  204.9 6.2 %collective-permute-start.48 = (bf16[32,1152]{1,0:T(8,128)(2,1)S(1)}, bf16[32,1152]{1,0:T(8,128)(2,1)S(1)}, u32[]{:S(2)}, u32[]{:S(2)}) collective-permute-start(bf16[32,1152]{1,0:T(8,128)(2,1)S(1)} %get-tuple-element.91), channel_id=1, source_target_pairs={{0,8},{4,12},{8,16},{12,20},{16,24},{20,28},{24,0},{28,4},{1,9},{5... | collective-permute-start | bytes 221192 | tf_op jit(solution)/shard_map/ppermute | solution.py:18
  206.3 18.5 %collective-permute-start.34 = (bf16[2,2,32,1024]{3,2,1,0:T(8,128)(2,1)S(1)}, bf16[2,2,32,1024]{3,2,1,0:T(8,128)(2,1)S(1)}, u32[]{:S(2)}, u32[]{:S(2)}) collective-permute-start(bf16[2,2,32,1024]{3,2,1,0:T(8,128)(2,1)S(1)} %slice_bitcast_fusion.2), channel_id=1, source_target_pairs={{0,1},{1,0},{2,3},{3,2},{4,5},{5,4},{6,7},{7,6},{8,9},{9,8},{10,11... | collective-permute-start | bytes 786440 | tf_op jit(solution)/shard_map/ppermute | solution.py:21
  206.9 10.3 %collective-permute-start.40 = (bf16[128,896]{1,0:T(8,128)(2,1)S(1)}, bf16[128,896]{1,0:T(8,128)(2,1)S(1)}, u32[]{:S(2)}, u32[]{:S(2)}) collective-permute-start(bf16[128,896]{1,0:T(8,128)(2,1)S(1)} %collective-permute-done.31), channel_id=1, source_target_pairs={{0,8},{4,12},{8,16},{12,20},{16,24},{20,28},{24,0},{28,4},{1,9},{5... | collective-permute-start | bytes 688136 | tf_op jit(solution)/shard_map/ppermute | solution.py:18
  211.0 10.0 %collective-permute-start.39 = (bf16[128,896]{1,0:T(8,128)(2,1)S(1)}, bf16[128,896]{1,0:T(8,128)(2,1)S(1)}, u32[]{:S(2)}, u32[]{:S(2)}) collective-permute-start(bf16[128,896]{1,0:T(8,128)(2,1)S(1)} %collective-permute-done.30), channel_id=1, source_target_pairs={{0,8},{4,12},{8,16},{12,20},{16,24},{20,28},{24,0},{28,4},{1,9},{5... | collective-permute-start | bytes 688136 | tf_op jit(solution)/shard_map/ppermute | solution.py:18
  224.9 5.6 %collective-permute-start.37 = (bf16[32,1024]{1,0:T(8,128)(2,1)S(1)}, bf16[32,1024]{1,0:T(8,128)(2,1)S(1)}, u32[]{:S(2)}, u32[]{:S(2)}) collective-permute-start(bf16[32,1024]{1,0:T(8,128)(2,1)S(1)} %get-tuple-element.77), channel_id=1, source_target_pairs={{0,6},{1,7},{2,4},{3,5},{4,2},{5,3},{6,0},{7,1},{8,14},{9,15},{10,... | collective-permute-start | bytes 196616 | tf_op jit(solution)/shard_map/ppermute | solution.py:34
  227.1 4.3 %collective-permute-start.36 = (bf16[32,1024]{1,0:T(8,128)(2,1)S(1)}, bf16[32,1024]{1,0:T(8,128)(2,1)S(1)}, u32[]{:S(2)}, u32[]{:S(2)}) collective-permute-start(bf16[32,1024]{1,0:T(8,128)(2,1)S(1)} %get-tuple-element.78), channel_id=1, source_target_pairs={{0,4},{1,5},{2,6},{3,7},{4,0},{5,1},{6,2},{7,3},{8,12},{9,13},{10,... | collective-permute-start | bytes 196616 | tf_op jit(solution)/shard_map/ppermute | solution.py:34
  227.5 4.3 %collective-permute-start.35 = (bf16[32,1024]{1,0:T(8,128)(2,1)S(1)}, bf16[32,1024]{1,0:T(8,128)(2,1)S(1)}, u32[]{:S(2)}, u32[]{:S(2)}) collective-permute-start(bf16[32,1024]{1,0:T(8,128)(2,1)S(1)} %get-tuple-element.76), channel_id=1, source_target_pairs={{0,2},{1,3},{2,0},{3,1},{4,6},{5,7},{6,4},{7,5},{8,10},{9,11},{10,... | collective-permute-start | bytes 196616 | tf_op jit(solution)/shard_map/ppermute | solution.py:34
  230.5 15.3 %collective-permute-start.29 = (bf16[32,1024]{1,0:T(8,128)(2,1)S(1)}, bf16[32,1024]{1,0:T(8,128)(2,1)S(1)}, u32[]{:S(2)}, u32[]{:S(2)}) collective-permute-start(bf16[32,1024]{1,0:T(8,128)(2,1)S(1)} %get-tuple-element.31), channel_id=1, source_target_pairs={{0,24},{4,28},{8,0},{12,4},{16,8},{20,12},{24,16},{28,20},{1,25},{... | collective-permute-start | bytes 196616 | tf_op jit(solution)/shard_map/ppermute | solution.py:18
  231.4 1.5 collective-permute-start.43
  233.0 5.2 %collective-permute-start.46 = (bf16[32,1024]{1,0:T(8,128)(2,1)S(1)}, bf16[32,1024]{1,0:T(8,128)(2,1)S(1)}, u32[]{:S(2)}, u32[]{:S(2)}) collective-permute-start(bf16[32,1024]{1,0:T(8,128)(2,1)S(1)} %get-tuple-element.74), channel_id=1, source_target_pairs={{0,6},{1,7},{2,4},{3,5},{4,2},{5,3},{6,0},{7,1},{8,14},{9,15},{10,... | collective-permute-start | bytes 196616 | tf_op jit(solution)/shard_map/ppermute | solution.py:34
  234.9 4.6 %collective-permute-start.45 = (bf16[32,1024]{1,0:T(8,128)(2,1)S(1)}, bf16[32,1024]{1,0:T(8,128)(2,1)S(1)}, u32[]{:S(2)}, u32[]{:S(2)}) collective-permute-start(bf16[32,1024]{1,0:T(8,128)(2,1)S(1)} %get-tuple-element.75), channel_id=1, source_target_pairs={{0,4},{1,5},{2,6},{3,7},{4,0},{5,1},{6,2},{7,3},{8,12},{9,13},{10,... | collective-permute-start | bytes 196616 | tf_op jit(solution)/shard_map/ppermute | solution.py:34
  235.7 4.3 %collective-permute-start.44 = (bf16[32,1024]{1,0:T(8,128)(2,1)S(1)}, bf16[32,1024]{1,0:T(8,128)(2,1)S(1)}, u32[]{:S(2)}, u32[]{:S(2)}) collective-permute-start(bf16[32,1024]{1,0:T(8,128)(2,1)S(1)} %get-tuple-element.73), channel_id=1, source_target_pairs={{0,2},{1,3},{2,0},{3,1},{4,6},{5,7},{6,4},{7,5},{8,10},{9,11},{10,... | collective-permute-start | bytes 196616 | tf_op jit(solution)/shard_map/ppermute | solution.py:34
  240.4 1.9 collective-permute-start.51
  240.6 32.1 %copy-start.6 = (f32[4096]{0:T(1024)S(1)}, f32[4096]{0:T(1024)}, u32[]{:S(2)}) copy-start(f32[4096]{0:T(1024)} %param.15) | copy-start | bytes 49156
  240.6 32.1 %copy-start.11 = (f32[32]{0:T(128)S(1)}, f32[32]{0:T(128)}, u32[]{:S(2)}) copy-start(f32[32]{0:T(128)} %copy-done.10) | copy-start | bytes 388
  241.1 32.9 %collective-permute-start.58 = (bf16[896,512]{1,0:T(8,128)(2,1)S(1)}, bf16[896,512]{1,0:T(8,128)(2,1)S(1)}, u32[]{:S(2)}, u32[]{:S(2)}) collective-permute-start(bf16[896,512]{1,0:T(8,128)(2,1)S(1)} %get-tuple-element.45), channel_id=1, source_target_pairs={{0,4},{4,0},{8,12},{12,8},{16,20},{20,16},{24,28},{28,24},{1,5},{5... | collective-permute-start | bytes 2752520 | tf_op jit(solution)/shard_map/ppermute | solution.py:24
  242.3 4.6 %collective-permute-start.54 = (f32[1024]{0:T(1024)S(1)}, f32[1024]{0:T(1024)S(1)}, u32[]{:S(2)}, u32[]{:S(2)}) collective-permute-start(f32[1024]{0:T(1024)S(1)} %add.404), channel_id=1, source_target_pairs={{0,6},{1,7},{2,4},{3,5},{4,2},{5,3},{6,0},{7,1},{8,14},{9,15},{10,... | collective-permute-start | bytes 12296 | tf_op jit(solution)/shard_map/ppermute | solution.py:34
  243.4 20.6 %collective-permute-start.53 = (f32[1024]{0:T(1024)S(1)}, f32[1024]{0:T(1024)S(1)}, u32[]{:S(2)}, u32[]{:S(2)}) collective-permute-start(f32[1024]{0:T(1024)S(1)} %add.404), channel_id=1, source_target_pairs={{0,4},{1,5},{2,6},{3,7},{4,0},{5,1},{6,2},{7,3},{8,12},{9,13},{10,... | collective-permute-start | bytes 12296 | tf_op jit(solution)/shard_map/ppermute | solution.py:34
  244.7 19.4 %collective-permute-start.52 = (f32[1024]{0:T(1024)S(1)}, f32[1024]{0:T(1024)S(1)}, u32[]{:S(2)}, u32[]{:S(2)}) collective-permute-start(f32[1024]{0:T(1024)S(1)} %add.404), channel_id=1, source_target_pairs={{0,2},{1,3},{2,0},{3,1},{4,6},{5,7},{6,4},{7,5},{8,10},{9,11},{10,... | collective-permute-start | bytes 12296 | tf_op jit(solution)/shard_map/ppermute | solution.py:34
  245.8 18.7 %collective-permute-start.38 = (bf16[32,1024]{1,0:T(8,128)(2,1)S(1)}, bf16[32,1024]{1,0:T(8,128)(2,1)S(1)}, u32[]{:S(2)}, u32[]{:S(2)}) collective-permute-start(bf16[32,1024]{1,0:T(8,128)(2,1)S(1)} %get-tuple-element.29), channel_id=1, source_target_pairs={{0,16},{4,20},{8,24},{12,28},{16,0},{20,4},{24,8},{28,12},{1,17},{... | collective-permute-start | bytes 196616 | tf_op jit(solution)/shard_map/ppermute | solution.py:18
  264.1 4.9 %collective-permute-start.55 = (f32[1024]{0:T(1024)S(1)}, f32[1024]{0:T(1024)S(1)}, u32[]{:S(2)}, u32[]{:S(2)}) collective-permute-start(f32[1024]{0:T(1024)S(1)} %get-tuple-element.26), channel_id=1, source_target_pairs={{0,24},{4,28},{8,0},{12,4},{16,8},{20,12},{24,16},{28,20},{1,25},{... | collective-permute-start | bytes 12296 | tf_op jit(solution)/shard_map/ppermute | solution.py:18
  264.5 8.2 %collective-permute-start.47 = (bf16[32,1024]{1,0:T(8,128)(2,1)S(1)}, bf16[32,1024]{1,0:T(8,128)(2,1)S(1)}, u32[]{:S(2)}, u32[]{:S(2)}) collective-permute-start(bf16[32,1024]{1,0:T(8,128)(2,1)S(1)} %get-tuple-element.27), channel_id=1, source_target_pairs={{0,8},{4,12},{8,16},{12,20},{16,24},{20,28},{24,0},{28,4},{1,9},{5... | collective-permute-start | bytes 196616 | tf_op jit(solution)/shard_map/ppermute | solution.py:18
  266.2 4.5 %collective-permute-start.56 = (f32[1024]{0:T(1024)S(1)}, f32[1024]{0:T(1024)S(1)}, u32[]{:S(2)}, u32[]{:S(2)}) collective-permute-start(f32[1024]{0:T(1024)S(1)} %get-tuple-element.26), channel_id=1, source_target_pairs={{0,16},{4,20},{8,24},{12,28},{16,0},{20,4},{24,8},{28,12},{1,17},{... | collective-permute-start | bytes 12296 | tf_op jit(solution)/shard_map/ppermute | solution.py:18
  266.6 5.4 %collective-permute-start.57 = (f32[1024]{0:T(1024)S(1)}, f32[1024]{0:T(1024)S(1)}, u32[]{:S(2)}, u32[]{:S(2)}) collective-permute-start(f32[1024]{0:T(1024)S(1)} %get-tuple-element.26), channel_id=1, source_target_pairs={{0,8},{4,12},{8,16},{12,20},{16,24},{20,28},{24,0},{28,4},{1,9},{5... | collective-permute-start | bytes 12296 | tf_op jit(solution)/shard_map/ppermute | solution.py:18
  (7 other events, 8.9 us)

commit v2 on v1

--- a/solution.py
+++ b/solution.py
@@ -185,11 +185,15 @@
             preferred_element_type=F32,
         ).astype(BF16)
         low, high = down_both[:, :own], down_both[:, own:]
-        theirs = move_pair(jnp.where(first, high, low))
+        give = jnp.where(first, high, low)
+        cut = hidden * 3 // 4 // 16 * 16
+        theirs = move_pair(give[:cut]), move_pair(give[cut:])
         down_grad = jnp.zeros((2 * hidden, own), BF16)
         mine = jnp.where(first, low, high)
         down_grad = lax.dynamic_update_slice_in_dim(down_grad, mine, b * hidden, 0)
-        down_grad = lax.dynamic_update_slice_in_dim(down_grad, theirs, (1 - b) * hidden, 0)
+        there = (1 - b) * hidden
+        down_grad = lax.dynamic_update_slice_in_dim(down_grad, theirs[0], there, 0)
+        down_grad = lax.dynamic_update_slice_in_dim(down_grad, theirs[1], there + cut, 0)
 
         gain = gain_part + move_core(gain_part)
         gain_sum = gain

time: 276 us -> 277 us (level)
  starting transfers between devices: 51.5 us -> 54.7 us
    ppermute x18, waiting for transfers between devices: 66.9 us -> 61.4 us  [move_br(): return lax.ppermute(value, ('dp', 'tensor'), pairs)]
    ppermute x30, waiting for transfers between devices: 98.3 us -> 103 us  [move_a(): return lax.ppermute(value, 'dp', ring(k % na))]
    ppermute x30, starting transfers between devices: 23.2 us -> 26.1 us  [move_a(): return lax.ppermute(value, 'dp', ring(k % na))]
    ppermute x4 -> x5, starting transfers between devices: 5.67 us -> 6.6 us  [move_pair(): return lax.ppermute(value, 'dp', [(d, d ^ 1) for d in range(groups)])]
  transfers between devices with their start and end apart: 59 -> 60, of which waited for: 34 -> 32; matrix products, arithmetic and copies ran while one was open for 17% -> 16% of each run, Pallas kernels for 0% -> 0%
where the time goes in v2:
time: 277 us
  waiting for transfers between devices  170 us (61%)
  starting transfers between devices  54.7 us (20%)
  other arithmetic  19.6 us (7%)
  matrix products  17.4 us (6%)
  local copies, waits for them, and re-layouts  13.7 us (5%)
    ppermute x30, waiting for transfers between devices, move_a(): return lax.ppermute(value, 'dp', ring(k % na))  103 us
    ppermute x18, waiting for transfers between devices, move_br(): return lax.ppermute(value, ('dp', 'tensor'), pairs)  61.4 us
    ppermute x30, starting transfers between devices, move_a(): return lax.ppermute(value, 'dp', ring(k % na))  26.1 us
    ppermute x18, starting transfers between devices, move_br(): return lax.ppermute(value, ('dp', 'tensor'), pairs)  21.2 us
    dot_general x4, matrix products, per_device(): jnp.einsum('grf,gdf->rd', jnp.stack((grad_gate, grad_up)), weight_pair, p...  12.7 us
    ppermute x5, starting transfers between devices, move_pair(): return lax.ppermute(value, 'dp', [(d, d ^ 1) for d in range(groups)])  6.6 us
  transfers between devices with their start and end apart: 60, of which 32 were waited for; matrix products, arithmetic and copies ran while one was open for 16% of the time, Pallas kernels for 0%

profile of v2, /device:TPU:0, one launch (start us, length us, event | category | flops | bytes accessed | tf_op | source)
XLA Modules:
  0.0 276.7 jit_solution(11217476568691552011)
XLA Ops:
  0.6 2.3 select_bitcast_fusion
  3.0 1.4 pad_maximum_fusion.1
  4.4 3.0 %collective-permute-start.16 = (bf16[2,512,896]{2,1,0:T(8,128)(2,1)}, bf16[2,512,896]{2,1,0:T(8,128)(2,1)}, u32[]{:S(2)}, u32[]{:S(2)}) collective-permute-start(bf16[2,512,896]{2,1,0:T(8,128)(2,1)} %pad_maximum_fusion.1), channel_id=1, source_target_pairs={{0,4},{4,0},{8,12},{12,8},{16,20},{20,16},{24,28},{28,24},{1,5},{5... | collective-permute-start | bytes 5505032 | tf_op jit(solution)/shard_map/ppermute | solution.py:24
  9.2 3.6 %collective-permute-start.2 = (bf16[32,1024]{1,0:T(8,128)(2,1)}, bf16[32,1024]{1,0:T(8,128)(2,1)S(1)}, u32[]{:S(2)}, u32[]{:S(2)}) collective-permute-start(bf16[32,1024]{1,0:T(8,128)(2,1)} %get-tuple-element.89), channel_id=1, source_target_pairs={{0,24},{4,28},{8,0},{12,4},{16,8},{20,12},{24,16},{28,20},{1,25},{... | collective-permute-start | bytes 196616 | tf_op jit(solution)/shard_map/ppermute | solution.py:18
  12.8 1.0 collective-permute-start
  18.0 2.8 %dynamic-slice_bitcast_fusion.1 = (bf16[896,512]{1,0:T(8,128)(2,1)}, bf16[896,512]{1,0:T(8,128)(2,1)}) fusion(bf16[2,896,512]{2,1,0:T(8,128)(2,1)} %bitcast.276, s32[]{:T(128)S(6)} %select_n.198, s32[]{:T(128)S(6)} %select_n.199), kind=kLoop, calls=%fused_computation.103 | loop fusion | bytes 3670024 | tf_op jit(solution)/shard_map/jit(dynamic_index_in_dim)/squeeze | solution.py:60
  21.5 1.7 fusion.94
  23.2 2.3 collective-permute-start.10
  26.7 2.1 broadcast_in_dim.13
  28.8 1.4 maximum_dynamic-update-slice_fusion
  30.2 3.4 %collective-permute-done.10 = bf16[4,32,1024]{2,1,0:T(8,128)(2,1)} collective-permute-done((bf16[4,32,1024]{2,1,0:T(8,128)(2,1)}, bf16[4,32,1024]{2,1,0:T(8,128)(2,1)}, u32[]{:S(2)}, u32[]{:S(2)}) %collective-permute-start.10) | collective-permute-done | bytes 262176 | tf_op jit(solution)/shard_map/ppermute | solution.py:34
  33.6 1.4 collective-permute-start.5
  35.0 34.7 %collective-permute-done.9 = bf16[4,32,1024]{2,1,0:T(8,128)(2,1)} collective-permute-done((bf16[4,32,1024]{2,1,0:T(8,128)(2,1)}, bf16[4,32,1024]{2,1,0:T(8,128)(2,1)}, u32[]{:S(2)}, u32[]{:S(2)}) %collective-permute-start.9) | collective-permute-done | bytes 262176 | tf_op jit(solution)/shard_map/ppermute | solution.py:34
  69.7 2.1 collective-permute-start.23
  71.7 1.1 fusion.92
  72.9 1.0 fusion.93
  74.5 1.1 maximum_convert_fusion
  76.0 6.3 %collective-permute-done.23 = bf16[2,128,896]{2,1,0:T(8,128)(2,1)S(1)} collective-permute-done((bf16[2,128,896]{2,1,0:T(8,128)(2,1)S(1)}, bf16[2,128,896]{2,1,0:T(8,128)(2,1)S(1)}, u32[]{:S(2)}, u32[]{:S(2)}) %collective-permute-start.23) | collective-permute-done | bytes 458784 | tf_op jit(solution)/shard_map/ppermute | solution.py:18
  82.3 1.5 collective-permute-start.32
  84.3 4.1 %collective-permute-done.5 = bf16[896,512]{1,0:T(8,128)(2,1)S(1)} collective-permute-done((bf16[896,512]{1,0:T(8,128)(2,1)}, bf16[896,512]{1,0:T(8,128)(2,1)S(1)}, u32[]{:S(2)}, u32[]{:S(2)}) %collective-permute-start.5) | collective-permute-done | bytes 917536 | tf_op jit(solution)/shard_map/ppermute | solution.py:24
  88.4 1.3 convolution_convert_fusion
  89.7 1.9 collective-permute-start.12
  91.6 1.3 convolution_convert_fusion.1
  92.9 1.6 collective-permute-start.6
  94.5 3.2 %collective-permute-done.24 = bf16[2,128,896]{2,1,0:T(8,128)(2,1)S(1)} collective-permute-done((bf16[2,128,896]{2,1,0:T(8,128)(2,1)}, bf16[2,128,896]{2,1,0:T(8,128)(2,1)S(1)}, u32[]{:S(2)}, u32[]{:S(2)}) %collective-permute-start.24) | collective-permute-done | bytes 458784 | tf_op jit(solution)/shard_map/ppermute | solution.py:18
  97.8 9.7 %collective-permute-done.32 = bf16[2,128,896]{2,1,0:T(8,128)(2,1)S(1)} collective-permute-done((bf16[2,128,896]{2,1,0:T(8,128)(2,1)S(1)}, bf16[2,128,896]{2,1,0:T(8,128)(2,1)S(1)}, u32[]{:S(2)}, u32[]{:S(2)}) %collective-permute-start.32) | collective-permute-done | bytes 458784 | tf_op jit(solution)/shard_map/ppermute | solution.py:18
  107.8 4.6 %collective-permute-done.12 = bf16[128,896]{1,0:T(8,128)(2,1)S(1)} collective-permute-done((bf16[128,896]{1,0:T(8,128)(2,1)S(1)}, bf16[128,896]{1,0:T(8,128)(2,1)S(1)}, u32[]{:S(2)}, u32[]{:S(2)}) %collective-permute-start.12) | collective-permute-done | bytes 229408 | tf_op jit(solution)/shard_map/ppermute | solution.py:18
  112.6 4.8 %collective-permute-done.6 = bf16[128,896]{1,0:T(8,128)(2,1)S(1)} collective-permute-done((bf16[128,896]{1,0:T(8,128)(2,1)S(1)}, bf16[128,896]{1,0:T(8,128)(2,1)S(1)}, u32[]{:S(2)}, u32[]{:S(2)}) %collective-permute-start.6) | collective-permute-done | bytes 229408 | tf_op jit(solution)/shard_map/ppermute | solution.py:18
  117.5 24.5 %collective-permute-done.13 = bf16[128,896]{1,0:T(8,128)(2,1)S(1)} collective-permute-done((bf16[128,896]{1,0:T(8,128)(2,1)S(1)}, bf16[128,896]{1,0:T(8,128)(2,1)S(1)}, u32[]{:S(2)}, u32[]{:S(2)}) %collective-permute-start.13) | collective-permute-done | bytes 229408 | tf_op jit(solution)/shard_map/ppermute | solution.py:18
  142.1 4.8 %collective-permute-done.7 = bf16[128,896]{1,0:T(8,128)(2,1)S(1)} collective-permute-done((bf16[128,896]{1,0:T(8,128)(2,1)S(1)}, bf16[128,896]{1,0:T(8,128)(2,1)S(1)}, u32[]{:S(2)}, u32[]{:S(2)}) %collective-permute-start.7) | collective-permute-done | bytes 229408 | tf_op jit(solution)/shard_map/ppermute | solution.py:18
  147.5 5.0 %collective-permute-done.14 = bf16[128,896]{1,0:T(8,128)(2,1)S(1)} collective-permute-done((bf16[128,896]{1,0:T(8,128)(2,1)S(1)}, bf16[128,896]{1,0:T(8,128)(2,1)S(1)}, u32[]{:S(2)}, u32[]{:S(2)}) %collective-permute-start.14) | collective-permute-done | bytes 229408 | tf_op jit(solution)/shard_map/ppermute | solution.py:18
  152.6 4.9 %collective-permute-done.8 = bf16[128,896]{1,0:T(8,128)(2,1)S(1)} collective-permute-done((bf16[128,896]{1,0:T(8,128)(2,1)S(1)}, bf16[128,896]{1,0:T(8,128)(2,1)S(1)}, u32[]{:S(2)}, u32[]{:S(2)}) %collective-permute-start.8) | collective-permute-done | bytes 229408 | tf_op jit(solution)/shard_map/ppermute | solution.py:18
  158.2 4.0 %collective-permute-start.50 = (bf16[32,1152]{1,0:T(8,128)(2,1)S(1)}, bf16[32,1152]{1,0:T(8,128)(2,1)S(1)}, u32[]{:S(2)}, u32[]{:S(2)}) collective-permute-start(bf16[32,1152]{1,0:T(8,128)(2,1)S(1)} %get-tuple-element.93), channel_id=1, source_target_pairs={{0,24},{4,28},{8,0},{12,4},{16,8},{20,12},{24,16},{28,20},{1,25},{... | collective-permute-start | bytes 221192 | tf_op jit(solution)/shard_map/ppermute | solution.py:18
  162.3 5.0 %collective-permute-done.42 = bf16[2,128,896]{2,1,0:T(8,128)(2,1)S(1)} collective-permute-done((bf16[2,128,896]{2,1,0:T(8,128)(2,1)S(1)}, bf16[2,128,896]{2,1,0:T(8,128)(2,1)S(1)}, u32[]{:S(2)}, u32[]{:S(2)}) %collective-permute-start.42) | collective-permute-done | bytes 458784 | tf_op jit(solution)/shard_map/ppermute | solution.py:18
  167.7 2.1 fusion.8
  170.5 2.9 %constant_dynamic-update-slice_fusion.16 = bf16[2,1024,896]{2,1,0:T(8,128)(2,1)} fusion(bf16[2,1024,896]{2,1,0:T(8,128)(2,1)} %maximum_dynamic-update-slice_fusion, bf16[2,512,896]{2,1,0:T(8,128)(2,1)} %collective-permute-done.16, s32[]{:T(128)S(6)} %select_n.220), kind=kLoop, calls=%fused_computation.237 | loop fusion | bytes 3670020 | tf_op jit(solution)/shard_map/dynamic_update_slice | solution.py:108
  173.4 3.2 %fusion.11 = bf16[256,1024]{1,0:T(8,128)(2,1)S(1)} fusion(bf16[2,1024,896]{2,1,0:T(8,128)(2,1)} %constant_dynamic-update-slice_fusion.16, bf16[1,256,896]{2,1,0:T(8,128)(2,1)S(1)} %get-tuple-element.44, bf16[1,256,896]{2,1,0:T(8,128)(2,1)S(1)} %get-tuple-element.43), kind=kOutput, calls=%fused_computation.19 | convolution fusion | flops 940244992 | bytes 5111808 | tf_op jit(solution)/shard_map/grf,gdf->rd/dot_general | solution.py:152
  177.3 3.2 %fusion.12 = bf16[256,1024]{1,0:T(8,128)(2,1)S(1)} fusion(bf16[2,1024,896]{2,1,0:T(8,128)(2,1)} %constant_dynamic-update-slice_fusion.16, bf16[1,256,896]{2,1,0:T(8,128)(2,1)S(1)} %get-tuple-element.42, bf16[1,256,896]{2,1,0:T(8,128)(2,1)S(1)} %get-tuple-element.41), kind=kOutput, calls=%fused_computation.20 | convolution fusion | flops 940244992 | bytes 5111808 | tf_op jit(solution)/shard_map/grf,gdf->rd/dot_general | solution.py:152
  180.5 3.5 %collective-permute-start.30 = (bf16[128,896]{1,0:T(8,128)(2,1)S(1)}, bf16[128,896]{1,0:T(8,128)(2,1)S(1)}, u32[]{:S(2)}, u32[]{:S(2)}) collective-permute-start(bf16[128,896]{1,0:T(8,128)(2,1)S(1)} %collective-permute-done.21), channel_id=1, source_target_pairs={{0,8},{4,12},{8,16},{12,20},{16,24},{20,28},{24,0},{28,4},{1,9},{5... | collective-permute-start | bytes 688136 | tf_op jit(solution)/shard_map/ppermute | solution.py:18
  184.0 6.8 %collective-permute-done.31 = bf16[128,896]{1,0:T(8,128)(2,1)S(1)} collective-permute-done((bf16[128,896]{1,0:T(8,128)(2,1)S(1)}, bf16[128,896]{1,0:T(8,128)(2,1)S(1)}, u32[]{:S(2)}, u32[]{:S(2)}) %collective-permute-start.31) | collective-permute-done | bytes 229408 | tf_op jit(solution)/shard_map/ppermute | solution.py:18
  190.8 4.4 %collective-permute-done.30 = bf16[128,896]{1,0:T(8,128)(2,1)S(1)} collective-permute-done((bf16[128,896]{1,0:T(8,128)(2,1)S(1)}, bf16[128,896]{1,0:T(8,128)(2,1)S(1)}, u32[]{:S(2)}, u32[]{:S(2)}) %collective-permute-start.30) | collective-permute-done | bytes 229408 | tf_op jit(solution)/shard_map/ppermute | solution.py:18
  195.8 3.2 %fusion.13 = bf16[256,1024]{1,0:T(8,128)(2,1)S(1)} fusion(bf16[2,1024,896]{2,1,0:T(8,128)(2,1)} %constant_dynamic-update-slice_fusion.16, bf16[1,256,896]{2,1,0:T(8,128)(2,1)S(1)} %get-tuple-element.40, bf16[1,256,896]{2,1,0:T(8,128)(2,1)S(1)} %get-tuple-element.39), kind=kOutput, calls=%fused_computation.21 | convolution fusion | flops 940244992 | bytes 5111808 | tf_op jit(solution)/shard_map/grf,gdf->rd/dot_general | solution.py:152
  199.1 2.5 collective-permute-start.20
  202.8 1.7 collective-permute-done.20
  204.5 2.5 collective-permute-start.28
  208.0 2.2 collective-permute-done.28
  213.1 4.2 %collective-permute-done.48 = bf16[32,1152]{1,0:T(8,128)(2,1)S(1)} collective-permute-done((bf16[32,1152]{1,0:T(8,128)(2,1)S(1)}, bf16[32,1152]{1,0:T(8,128)(2,1)S(1)}, u32[]{:S(2)}, u32[]{:S(2)}) %collective-permute-start.48) | collective-permute-done | bytes 73760 | tf_op jit(solution)/shard_map/ppermute | solution.py:18
  217.7 7.0 %collective-permute-done.29 = bf16[32,1024]{1,0:T(8,128)(2,1)S(1)} collective-permute-done((bf16[32,1024]{1,0:T(8,128)(2,1)S(1)}, bf16[32,1024]{1,0:T(8,128)(2,1)S(1)}, u32[]{:S(2)}, u32[]{:S(2)}) %collective-permute-start.29) | collective-permute-done | bytes 65568 | tf_op jit(solution)/shard_map/ppermute | solution.py:18
  225.3 3.2 %fusion.14 = bf16[256,1024]{1,0:T(8,128)(2,1)S(1)} fusion(bf16[2,1024,896]{2,1,0:T(8,128)(2,1)} %constant_dynamic-update-slice_fusion.16, bf16[1,256,896]{2,1,0:T(8,128)(2,1)S(1)} %get-tuple-element.38, bf16[1,256,896]{2,1,0:T(8,128)(2,1)S(1)} %get-tuple-element.37), kind=kOutput, calls=%fused_computation.22 | convolution fusion | flops 940244992 | bytes 5111808 | tf_op jit(solution)/shard_map/grf,gdf->rd/dot_general | solution.py:152
  228.6 2.0 collective-permute-start.37
  232.2 2.0 collective-permute-done.37
  234.1 1.1 collective-permute-start.58
  235.7 1.3 collective-permute-done.43
  237.1 1.8 collective-permute-start.46
  238.9 1.3 collective-permute-start.45
  240.7 1.6 collective-permute-done.46
  242.3 1.1 collective-permute-start.59
  243.4 11.8 %collective-permute-done.45 = bf16[32,1024]{1,0:T(8,128)(2,1)S(1)} collective-permute-done((bf16[32,1024]{1,0:T(8,128)(2,1)S(1)}, bf16[32,1024]{1,0:T(8,128)(2,1)S(1)}, u32[]{:S(2)}, u32[]{:S(2)}) %collective-permute-start.45) | collective-permute-done | bytes 65568 | tf_op jit(solution)/shard_map/ppermute | solution.py:34
  256.2 4.8 %collective-permute-done.38 = bf16[32,1024]{1,0:T(8,128)(2,1)S(1)} collective-permute-done((bf16[32,1024]{1,0:T(8,128)(2,1)S(1)}, bf16[32,1024]{1,0:T(8,128)(2,1)S(1)}, u32[]{:S(2)}, u32[]{:S(2)}) %collective-permute-start.38) | collective-permute-done | bytes 65568 | tf_op jit(solution)/shard_map/ppermute | solution.py:18
  261.0 2.4 collective-permute-start.54
  265.6 1.5 collective-permute-done.53
  267.3 2.0 collective-permute-start.47
  269.4 2.4 collective-permute-start.57
  271.8 2.1 collective-permute-done.56
  (194 shorter events, 28.7 us)
Async XLA Ops:
  4.4 166.1 %collective-permute-start.16 = (bf16[2,512,896]{2,1,0:T(8,128)(2,1)}, bf16[2,512,896]{2,1,0:T(8,128)(2,1)}, u32[]{:S(2)}, u32[]{:S(2)}) collective-permute-start(bf16[2,512,896]{2,1,0:T(8,128)(2,1)} %pad_maximum_fusion.1), channel_id=1, source_target_pairs={{0,4},{4,0},{8,12},{12,8},{16,20},{20,16},{24,28},{28,24},{1,5},{5... | collective-permute-start | bytes 5505032 | tf_op jit(solution)/shard_map/ppermute | solution.py:24
  7.6 6.2 %copy-start = (bf16[32,4096]{1,0:T(8,128)(2,1)S(1)}, bf16[32,4096]{1,0:T(8,128)(2,1)}, u32[]{:S(2)}) copy-start(bf16[32,4096]{1,0:T(8,128)(2,1)} %param.8) | copy-start | bytes 786436
  7.8 66.2 %collective-permute-start.15 = (bf16[2,128,896]{2,1,0:T(8,128)(2,1)S(1)}, bf16[2,128,896]{2,1,0:T(8,128)(2,1)}, u32[]{:S(2)}, u32[]{:S(2)}) collective-permute-start(bf16[2,128,896]{2,1,0:T(8,128)(2,1)S(1)} %pad_maximum_fusion.9), channel_id=1, source_target_pairs={{0,4},{4,0},{8,12},{12,8},{16,20},{20,16},{24,28},{28,24},{1,5},{5... | collective-permute-start | bytes 1376264 | tf_op jit(solution)/shard_map/ppermute | solution.py:24
  9.2 11.7 %collective-permute-start.2 = (bf16[32,1024]{1,0:T(8,128)(2,1)}, bf16[32,1024]{1,0:T(8,128)(2,1)S(1)}, u32[]{:S(2)}, u32[]{:S(2)}) collective-permute-start(bf16[32,1024]{1,0:T(8,128)(2,1)} %get-tuple-element.89), channel_id=1, source_target_pairs={{0,24},{4,28},{8,0},{12,4},{16,8},{20,12},{24,16},{28,20},{1,25},{... | collective-permute-start | bytes 196616 | tf_op jit(solution)/shard_map/ppermute | solution.py:18
  12.8 8.1 %collective-permute-start.1 = (bf16[32,1024]{1,0:T(8,128)(2,1)}, bf16[32,1024]{1,0:T(8,128)(2,1)S(1)}, u32[]{:S(2)}, u32[]{:S(2)}) collective-permute-start(bf16[32,1024]{1,0:T(8,128)(2,1)} %get-tuple-element.90), channel_id=1, source_target_pairs={{0,16},{4,20},{8,24},{12,28},{16,0},{20,4},{24,8},{28,12},{1,17},{... | collective-permute-start | bytes 196616 | tf_op jit(solution)/shard_map/ppermute | solution.py:18
  12.8 8.1 %collective-permute-start = (bf16[32,1024]{1,0:T(8,128)(2,1)S(1)}, bf16[32,1024]{1,0:T(8,128)(2,1)S(1)}, u32[]{:S(2)}, u32[]{:S(2)}) collective-permute-start(bf16[32,1024]{1,0:T(8,128)(2,1)S(1)} %get-tuple-element.88), channel_id=1, source_target_pairs={{0,8},{4,12},{8,16},{12,20},{16,24},{20,28},{24,0},{28,4},{1,9},{5... | collective-permute-start | bytes 196616 | tf_op jit(solution)/shard_map/ppermute | solution.py:18
  23.2 10.4 %collective-permute-start.10 = (bf16[4,32,1024]{2,1,0:T(8,128)(2,1)}, bf16[4,32,1024]{2,1,0:T(8,128)(2,1)}, u32[]{:S(2)}, u32[]{:S(2)}) collective-permute-start(bf16[4,32,1024]{2,1,0:T(8,128)(2,1)} %get-tuple-element.86), channel_id=1, source_target_pairs={{0,6},{1,7},{2,4},{3,5},{4,2},{5,3},{6,0},{7,1},{8,14},{9,15},{10,... | collective-permute-start | bytes 786440 | tf_op jit(solution)/shard_map/ppermute | solution.py:34
  25.5 44.1 %collective-permute-start.9 = (bf16[4,32,1024]{2,1,0:T(8,128)(2,1)}, bf16[4,32,1024]{2,1,0:T(8,128)(2,1)}, u32[]{:S(2)}, u32[]{:S(2)}) collective-permute-start(bf16[4,32,1024]{2,1,0:T(8,128)(2,1)} %get-tuple-element.86), channel_id=1, source_target_pairs={{0,4},{1,5},{2,6},{3,7},{4,0},{5,1},{6,2},{7,3},{8,12},{9,13},{10,... | collective-permute-start | bytes 786440 | tf_op jit(solution)/shard_map/ppermute | solution.py:34
  26.2 46.7 %collective-permute-start.3 = (bf16[4,32,1024]{2,1,0:T(8,128)(2,1)}, bf16[4,32,1024]{2,1,0:T(8,128)(2,1)}, u32[]{:S(2)}, u32[]{:S(2)}) collective-permute-start(bf16[4,32,1024]{2,1,0:T(8,128)(2,1)} %get-tuple-element.86), channel_id=1, source_target_pairs={{0,2},{1,3},{2,0},{3,1},{4,6},{5,7},{6,4},{7,5},{8,10},{9,11},{10,... | collective-permute-start | bytes 786440 | tf_op jit(solution)/shard_map/ppermute | solution.py:34
  33.6 54.7 %collective-permute-start.5 = (bf16[896,512]{1,0:T(8,128)(2,1)}, bf16[896,512]{1,0:T(8,128)(2,1)S(1)}, u32[]{:S(2)}, u32[]{:S(2)}) collective-permute-start(bf16[896,512]{1,0:T(8,128)(2,1)} %get-tuple-element.48), channel_id=1, source_target_pairs={{0,4},{4,0},{8,12},{12,8},{16,20},{20,16},{24,28},{28,24},{1,5},{5... | collective-permute-start | bytes 2752520 | tf_op jit(solution)/shard_map/ppermute | solution.py:24
  69.7 12.6 %collective-permute-start.23 = (bf16[2,128,896]{2,1,0:T(8,128)(2,1)S(1)}, bf16[2,128,896]{2,1,0:T(8,128)(2,1)S(1)}, u32[]{:S(2)}, u32[]{:S(2)}) collective-permute-start(bf16[2,128,896]{2,1,0:T(8,128)(2,1)S(1)} %pad_maximum_fusion.8), channel_id=1, source_target_pairs={{0,8},{4,12},{8,16},{12,20},{16,24},{20,28},{24,0},{28,4},{1,9},{5... | collective-permute-start | bytes 1376264 | tf_op jit(solution)/shard_map/ppermute | solution.py:18
  72.9 9.5 %collective-permute-start.11 = (bf16[2,4,32,1024]{3,2,1,0:T(8,128)(2,1)S(1)}, bf16[2,4,32,1024]{3,2,1,0:T(8,128)(2,1)S(1)}, u32[]{:S(2)}, u32[]{:S(2)}) collective-permute-start(bf16[2,4,32,1024]{3,2,1,0:T(8,128)(2,1)S(1)} %get-tuple-element.56), channel_id=1, source_target_pairs={{0,1},{1,0},{2,3},{3,2},{4,5},{5,4},{6,7},{7,6},{8,9},{9,8},{10,11... | collective-permute-start | bytes 1572872 | tf_op jit(solution)/shard_map/ppermute | solution.py:21
  74.0 10.0 %collective-permute-start.4 = (bf16[2,4,32,1024]{3,2,0,1:T(8,128)(2,1)S(1)}, bf16[2,4,32,1024]{3,2,0,1:T(8,128)(2,1)S(1)}, u32[]{:S(2)}, u32[]{:S(2)}) collective-permute-start(bf16[2,4,32,1024]{3,2,0,1:T(8,128)(2,1)S(1)} %get-tuple-element.54), channel_id=1, source_target_pairs={{0,1},{1,0},{2,3},{3,2},{4,5},{5,4},{6,7},{7,6},{8,9},{9,8},{10,11... | collective-permute-start | bytes 1572872 | tf_op jit(solution)/shard_map/ppermute | solution.py:21
  82.3 15.4 %collective-permute-start.24 = (bf16[2,128,896]{2,1,0:T(8,128)(2,1)}, bf16[2,128,896]{2,1,0:T(8,128)(2,1)S(1)}, u32[]{:S(2)}, u32[]{:S(2)}) collective-permute-start(bf16[2,128,896]{2,1,0:T(8,128)(2,1)} %collective-permute-done.15), channel_id=1, source_target_pairs={{0,8},{4,12},{8,16},{12,20},{16,24},{20,28},{24,0},{28,4},{1,9},{5... | collective-permute-start | bytes 1376264 | tf_op jit(solution)/shard_map/ppermute | solution.py:18
  82.3 25.2 %collective-permute-start.32 = (bf16[2,128,896]{2,1,0:T(8,128)(2,1)S(1)}, bf16[2,128,896]{2,1,0:T(8,128)(2,1)S(1)}, u32[]{:S(2)}, u32[]{:S(2)}) collective-permute-start(bf16[2,128,896]{2,1,0:T(8,128)(2,1)S(1)} %collective-permute-done.23), channel_id=1, source_target_pairs={{0,8},{4,12},{8,16},{12,20},{16,24},{20,28},{24,0},{28,4},{1,9},{5... | collective-permute-start | bytes 1376264 | tf_op jit(solution)/shard_map/ppermute | solution.py:18
  89.7 22.7 %collective-permute-start.12 = (bf16[128,896]{1,0:T(8,128)(2,1)S(1)}, bf16[128,896]{1,0:T(8,128)(2,1)S(1)}, u32[]{:S(2)}, u32[]{:S(2)}) collective-permute-start(bf16[128,896]{1,0:T(8,128)(2,1)S(1)} %slice.308), channel_id=1, source_target_pairs={{0,8},{4,12},{8,16},{12,20},{16,24},{20,28},{24,0},{28,4},{1,9},{5... | collective-permute-start | bytes 688136 | tf_op jit(solution)/shard_map/ppermute | solution.py:18
  92.9 24.5 %collective-permute-start.6 = (bf16[128,896]{1,0:T(8,128)(2,1)S(1)}, bf16[128,896]{1,0:T(8,128)(2,1)S(1)}, u32[]{:S(2)}, u32[]{:S(2)}) collective-permute-start(bf16[128,896]{1,0:T(8,128)(2,1)S(1)} %slice.304), channel_id=1, source_target_pairs={{0,8},{4,12},{8,16},{12,20},{16,24},{20,28},{24,0},{28,4},{1,9},{5... | collective-permute-start | bytes 688136 | tf_op jit(solution)/shard_map/ppermute | solution.py:18
  97.7 49.3 %collective-permute-start.33 = (bf16[2,128,896]{2,1,0:T(8,128)(2,1)S(1)}, bf16[2,128,896]{2,1,0:T(8,128)(2,1)S(1)}, u32[]{:S(2)}, u32[]{:S(2)}) collective-permute-start(bf16[2,128,896]{2,1,0:T(8,128)(2,1)S(1)} %collective-permute-done.24), channel_id=1, source_target_pairs={{0,8},{4,12},{8,16},{12,20},{16,24},{20,28},{24,0},{28,4},{1,9},{5... | collective-permute-start | bytes 1376264 | tf_op jit(solution)/shard_map/ppermute | solution.py:18
  107.5 50.7 %collective-permute-start.41 = (bf16[2,128,896]{2,1,0:T(8,128)(2,1)S(1)}, bf16[2,128,896]{2,1,0:T(8,128)(2,1)S(1)}, u32[]{:S(2)}, u32[]{:S(2)}) collective-permute-start(bf16[2,128,896]{2,1,0:T(8,128)(2,1)S(1)} %collective-permute-done.32), channel_id=1, source_target_pairs={{0,8},{4,12},{8,16},{12,20},{16,24},{20,28},{24,0},{28,4},{1,9},{5... | collective-permute-start | bytes 1376264 | tf_op jit(solution)/shard_map/ppermute | solution.py:18
  112.5 29.4 %collective-permute-start.13 = (bf16[128,896]{1,0:T(8,128)(2,1)S(1)}, bf16[128,896]{1,0:T(8,128)(2,1)S(1)}, u32[]{:S(2)}, u32[]{:S(2)}) collective-permute-start(bf16[128,896]{1,0:T(8,128)(2,1)S(1)} %add_convert_fusion.2), channel_id=1, source_target_pairs={{0,8},{4,12},{8,16},{12,20},{16,24},{20,28},{24,0},{28,4},{1,9},{5... | collective-permute-start | bytes 688136 | tf_op jit(solution)/shard_map/ppermute | solution.py:18
  117.4 29.4 %collective-permute-start.7 = (bf16[128,896]{1,0:T(8,128)(2,1)S(1)}, bf16[128,896]{1,0:T(8,128)(2,1)S(1)}, u32[]{:S(2)}, u32[]{:S(2)}) collective-permute-start(bf16[128,896]{1,0:T(8,128)(2,1)S(1)} %add_convert_fusion.5), channel_id=1, source_target_pairs={{0,8},{4,12},{8,16},{12,20},{16,24},{20,28},{24,0},{28,4},{1,9},{5... | collective-permute-start | bytes 688136 | tf_op jit(solution)/shard_map/ppermute | solution.py:18
  142.0 10.4 %collective-permute-start.14 = (bf16[128,896]{1,0:T(8,128)(2,1)S(1)}, bf16[128,896]{1,0:T(8,128)(2,1)S(1)}, u32[]{:S(2)}, u32[]{:S(2)}) collective-permute-start(bf16[128,896]{1,0:T(8,128)(2,1)S(1)} %add_convert_fusion.1), channel_id=1, source_target_pairs={{0,8},{4,12},{8,16},{12,20},{16,24},{20,28},{24,0},{28,4},{1,9},{5... | collective-permute-start | bytes 688136 | tf_op jit(solution)/shard_map/ppermute | solution.py:18
  146.9 10.5 %collective-permute-start.8 = (bf16[128,896]{1,0:T(8,128)(2,1)S(1)}, bf16[128,896]{1,0:T(8,128)(2,1)S(1)}, u32[]{:S(2)}, u32[]{:S(2)}) collective-permute-start(bf16[128,896]{1,0:T(8,128)(2,1)S(1)} %add_convert_fusion.4), channel_id=1, source_target_pairs={{0,8},{4,12},{8,16},{12,20},{16,24},{20,28},{24,0},{28,4},{1,9},{5... | collective-permute-start | bytes 688136 | tf_op jit(solution)/shard_map/ppermute | solution.py:18
  147.1 20.1 %collective-permute-start.42 = (bf16[2,128,896]{2,1,0:T(8,128)(2,1)S(1)}, bf16[2,128,896]{2,1,0:T(8,128)(2,1)S(1)}, u32[]{:S(2)}, u32[]{:S(2)}) collective-permute-start(bf16[2,128,896]{2,1,0:T(8,128)(2,1)S(1)} %collective-permute-done.33), channel_id=1, source_target_pairs={{0,8},{4,12},{8,16},{12,20},{16,24},{20,28},{24,0},{28,4},{1,9},{5... | collective-permute-start | bytes 1376264 | tf_op jit(solution)/shard_map/ppermute | solution.py:18
  152.5 24.2 %collective-permute-start.22 = (bf16[128,896]{1,0:T(8,128)(2,1)S(1)}, bf16[128,896]{1,0:T(8,128)(2,1)S(1)}, u32[]{:S(2)}, u32[]{:S(2)}) collective-permute-start(bf16[128,896]{1,0:T(8,128)(2,1)S(1)} %add_convert_fusion), channel_id=1, source_target_pairs={{0,8},{4,12},{8,16},{12,20},{16,24},{20,28},{24,0},{28,4},{1,9},{5... | collective-permute-start | bytes 688136 | tf_op jit(solution)/shard_map/ppermute | solution.py:18
  157.5 19.2 %collective-permute-start.21 = (bf16[128,896]{1,0:T(8,128)(2,1)S(1)}, bf16[128,896]{1,0:T(8,128)(2,1)S(1)}, u32[]{:S(2)}, u32[]{:S(2)}) collective-permute-start(bf16[128,896]{1,0:T(8,128)(2,1)S(1)} %add_convert_fusion.3), channel_id=1, source_target_pairs={{0,8},{4,12},{8,16},{12,20},{16,24},{20,28},{24,0},{28,4},{1,9},{5... | collective-permute-start | bytes 688136 | tf_op jit(solution)/shard_map/ppermute | solution.py:18
  158.2 97.6 %collective-permute-start.50 = (bf16[32,1152]{1,0:T(8,128)(2,1)S(1)}, bf16[32,1152]{1,0:T(8,128)(2,1)S(1)}, u32[]{:S(2)}, u32[]{:S(2)}) collective-permute-start(bf16[32,1152]{1,0:T(8,128)(2,1)S(1)} %get-tuple-element.93), channel_id=1, source_target_pairs={{0,24},{4,28},{8,0},{12,4},{16,8},{20,12},{24,16},{28,20},{1,25},{... | collective-permute-start | bytes 221192 | tf_op jit(solution)/shard_map/ppermute | solution.py:18
  167.3 68.2 %collective-permute-start.49 = (bf16[32,1152]{1,0:T(8,128)(2,1)S(1)}, bf16[32,1152]{1,0:T(8,128)(2,1)S(1)}, u32[]{:S(2)}, u32[]{:S(2)}) collective-permute-start(bf16[32,1152]{1,0:T(8,128)(2,1)S(1)} %get-tuple-element.92), channel_id=1, source_target_pairs={{0,16},{4,20},{8,24},{12,28},{16,0},{20,4},{24,8},{28,12},{1,17},{... | collective-permute-start | bytes 221192 | tf_op jit(solution)/shard_map/ppermute | solution.py:18
  176.6 22.4 %collective-permute-start.17 = (bf16[2,2,32,1024]{3,2,1,0:T(8,128)(2,1)S(1)}, bf16[2,2,32,1024]{3,2,1,0:T(8,128)(2,1)S(1)}, u32[]{:S(2)}, u32[]{:S(2)}) collective-permute-start(bf16[2,2,32,1024]{3,2,1,0:T(8,128)(2,1)S(1)} %slice_bitcast_fusion.6), channel_id=1, source_target_pairs={{0,1},{1,0},{2,3},{3,2},{4,5},{5,4},{6,7},{7,6},{8,9},{9,8},{10,11... | collective-permute-start | bytes 786440 | tf_op jit(solution)/shard_map/ppermute | solution.py:21
  180.5 10.3 %collective-permute-start.31 = (bf16[128,896]{1,0:T(8,128)(2,1)S(1)}, bf16[128,896]{1,0:T(8,128)(2,1)S(1)}, u32[]{:S(2)}, u32[]{:S(2)}) collective-permute-start(bf16[128,896]{1,0:T(8,128)(2,1)S(1)} %collective-permute-done.22), channel_id=1, source_target_pairs={{0,8},{4,12},{8,16},{12,20},{16,24},{20,28},{24,0},{28,4},{1,9},{5... | collective-permute-start | bytes 688136 | tf_op jit(solution)/shard_map/ppermute | solution.py:18
  180.5 14.7 %collective-permute-start.30 = (bf16[128,896]{1,0:T(8,128)(2,1)S(1)}, bf16[128,896]{1,0:T(8,128)(2,1)S(1)}, u32[]{:S(2)}, u32[]{:S(2)}) collective-permute-start(bf16[128,896]{1,0:T(8,128)(2,1)S(1)} %collective-permute-done.21), channel_id=1, source_target_pairs={{0,8},{4,12},{8,16},{12,20},{16,24},{20,28},{24,0},{28,4},{1,9},{5... | collective-permute-start | bytes 688136 | tf_op jit(solution)/shard_map/ppermute | solution.py:18
  190.8 11.3 %collective-permute-start.25 = (bf16[2,2,32,1024]{3,2,1,0:T(8,128)(2,1)S(1)}, bf16[2,2,32,1024]{3,2,1,0:T(8,128)(2,1)S(1)}, u32[]{:S(2)}, u32[]{:S(2)}) collective-permute-start(bf16[2,2,32,1024]{3,2,1,0:T(8,128)(2,1)S(1)} %slice_bitcast_fusion.4), channel_id=1, source_target_pairs={{0,1},{1,0},{2,3},{3,2},{4,5},{5,4},{6,7},{7,6},{8,9},{9,8},{10,11... | collective-permute-start | bytes 786440 | tf_op jit(solution)/shard_map/ppermute | solution.py:21
  199.1 5.3 %collective-permute-start.20 = (bf16[32,1024]{1,0:T(8,128)(2,1)S(1)}, bf16[32,1024]{1,0:T(8,128)(2,1)S(1)}, u32[]{:S(2)}, u32[]{:S(2)}) collective-permute-start(bf16[32,1024]{1,0:T(8,128)(2,1)S(1)} %get-tuple-element.83), channel_id=1, source_target_pairs={{0,6},{1,7},{2,4},{3,5},{4,2},{5,3},{6,0},{7,1},{8,14},{9,15},{10,... | collective-permute-start | bytes 196616 | tf_op jit(solution)/shard_map/ppermute | solution.py:34
  201.6 5.3 %collective-permute-start.19 = (bf16[32,1024]{1,0:T(8,128)(2,1)S(1)}, bf16[32,1024]{1,0:T(8,128)(2,1)S(1)}, u32[]{:S(2)}, u32[]{:S(2)}) collective-permute-start(bf16[32,1024]{1,0:T(8,128)(2,1)S(1)} %get-tuple-element.84), channel_id=1, source_target_pairs={{0,4},{1,5},{2,6},{3,7},{4,0},{5,1},{6,2},{7,3},{8,12},{9,13},{10,... | collective-permute-start | bytes 196616 | tf_op jit(solution)/shard_map/ppermute | solution.py:34
  202.1 5.8 %collective-permute-start.18 = (bf16[32,1024]{1,0:T(8,128)(2,1)S(1)}, bf16[32,1024]{1,0:T(8,128)(2,1)S(1)}, u32[]{:S(2)}, u32[]{:S(2)}) collective-permute-start(bf16[32,1024]{1,0:T(8,128)(2,1)S(1)} %get-tuple-element.82), channel_id=1, source_target_pairs={{0,2},{1,3},{2,0},{3,1},{4,6},{5,7},{6,4},{7,5},{8,10},{9,11},{10,... | collective-permute-start | bytes 196616 | tf_op jit(solution)/shard_map/ppermute | solution.py:34
  204.5 5.7 %collective-permute-start.28 = (bf16[32,1024]{1,0:T(8,128)(2,1)S(1)}, bf16[32,1024]{1,0:T(8,128)(2,1)S(1)}, u32[]{:S(2)}, u32[]{:S(2)}) collective-permute-start(bf16[32,1024]{1,0:T(8,128)(2,1)S(1)} %get-tuple-element.80), channel_id=1, source_target_pairs={{0,6},{1,7},{2,4},{3,5},{4,2},{5,3},{6,0},{7,1},{8,14},{9,15},{10,... | collective-permute-start | bytes 196616 | tf_op jit(solution)/shard_map/ppermute | solution.py:34
  207.0 4.3 %collective-permute-start.27 = (bf16[32,1024]{1,0:T(8,128)(2,1)S(1)}, bf16[32,1024]{1,0:T(8,128)(2,1)S(1)}, u32[]{:S(2)}, u32[]{:S(2)}) collective-permute-start(bf16[32,1024]{1,0:T(8,128)(2,1)S(1)} %get-tuple-element.81), channel_id=1, source_target_pairs={{0,4},{1,5},{2,6},{3,7},{4,0},{5,1},{6,2},{7,3},{8,12},{9,13},{10,... | collective-permute-start | bytes 196616 | tf_op jit(solution)/shard_map/ppermute | solution.py:34
  207.9 4.3 %collective-permute-start.26 = (bf16[32,1024]{1,0:T(8,128)(2,1)S(1)}, bf16[32,1024]{1,0:T(8,128)(2,1)S(1)}, u32[]{:S(2)}, u32[]{:S(2)}) collective-permute-start(bf16[32,1024]{1,0:T(8,128)(2,1)S(1)} %get-tuple-element.79), channel_id=1, source_target_pairs={{0,2},{1,3},{2,0},{3,1},{4,6},{5,7},{6,4},{7,5},{8,10},{9,11},{10,... | collective-permute-start | bytes 196616 | tf_op jit(solution)/shard_map/ppermute | solution.py:34
  210.2 7.1 %collective-permute-start.48 = (bf16[32,1152]{1,0:T(8,128)(2,1)S(1)}, bf16[32,1152]{1,0:T(8,128)(2,1)S(1)}, u32[]{:S(2)}, u32[]{:S(2)}) collective-permute-start(bf16[32,1152]{1,0:T(8,128)(2,1)S(1)} %get-tuple-element.91), channel_id=1, source_target_pairs={{0,8},{4,12},{8,16},{12,20},{16,24},{20,28},{24,0},{28,4},{1,9},{5... | collective-permute-start | bytes 221192 | tf_op jit(solution)/shard_map/ppermute | solution.py:18
  211.2 13.5 %collective-permute-start.40 = (bf16[128,896]{1,0:T(8,128)(2,1)S(1)}, bf16[128,896]{1,0:T(8,128)(2,1)S(1)}, u32[]{:S(2)}, u32[]{:S(2)}) collective-permute-start(bf16[128,896]{1,0:T(8,128)(2,1)S(1)} %collective-permute-done.31), channel_id=1, source_target_pairs={{0,8},{4,12},{8,16},{12,20},{16,24},{20,28},{24,0},{28,4},{1,9},{5... | collective-permute-start | bytes 688136 | tf_op jit(solution)/shard_map/ppermute | solution.py:18
  212.2 12.5 %collective-permute-start.39 = (bf16[128,896]{1,0:T(8,128)(2,1)S(1)}, bf16[128,896]{1,0:T(8,128)(2,1)S(1)}, u32[]{:S(2)}, u32[]{:S(2)}) collective-permute-start(bf16[128,896]{1,0:T(8,128)(2,1)S(1)} %collective-permute-done.30), channel_id=1, source_target_pairs={{0,8},{4,12},{8,16},{12,20},{16,24},{20,28},{24,0},{28,4},{1,9},{5... | collective-permute-start | bytes 688136 | tf_op jit(solution)/shard_map/ppermute | solution.py:18
  217.3 7.4 %collective-permute-start.29 = (bf16[32,1024]{1,0:T(8,128)(2,1)S(1)}, bf16[32,1024]{1,0:T(8,128)(2,1)S(1)}, u32[]{:S(2)}, u32[]{:S(2)}) collective-permute-start(bf16[32,1024]{1,0:T(8,128)(2,1)S(1)} %get-tuple-element.31), channel_id=1, source_target_pairs={{0,24},{4,28},{8,0},{12,4},{16,8},{20,12},{24,16},{28,20},{1,25},{... | collective-permute-start | bytes 196616 | tf_op jit(solution)/shard_map/ppermute | solution.py:18
  224.7 3.8 %collective-permute-start.34 = (bf16[2,2,32,1024]{3,2,1,0:T(8,128)(2,1)S(1)}, bf16[2,2,32,1024]{3,2,1,0:T(8,128)(2,1)S(1)}, u32[]{:S(2)}, u32[]{:S(2)}) collective-permute-start(bf16[2,2,32,1024]{3,2,1,0:T(8,128)(2,1)S(1)} %slice_bitcast_fusion.2), channel_id=1, source_target_pairs={{0,1},{1,0},{2,3},{3,2},{4,5},{5,4},{6,7},{7,6},{8,9},{9,8},{10,11... | collective-permute-start | bytes 786440 | tf_op jit(solution)/shard_map/ppermute | solution.py:21
  228.6 5.5 %collective-permute-start.37 = (bf16[32,1024]{1,0:T(8,128)(2,1)S(1)}, bf16[32,1024]{1,0:T(8,128)(2,1)S(1)}, u32[]{:S(2)}, u32[]{:S(2)}) collective-permute-start(bf16[32,1024]{1,0:T(8,128)(2,1)S(1)} %get-tuple-element.77), channel_id=1, source_target_pairs={{0,6},{1,7},{2,4},{3,5},{4,2},{5,3},{6,0},{7,1},{8,14},{9,15},{10,... | collective-permute-start | bytes 196616 | tf_op jit(solution)/shard_map/ppermute | solution.py:34
  230.6 4.8 %collective-permute-start.36 = (bf16[32,1024]{1,0:T(8,128)(2,1)S(1)}, bf16[32,1024]{1,0:T(8,128)(2,1)S(1)}, u32[]{:S(2)}, u32[]{:S(2)}) collective-permute-start(bf16[32,1024]{1,0:T(8,128)(2,1)S(1)} %get-tuple-element.78), channel_id=1, source_target_pairs={{0,4},{1,5},{2,6},{3,7},{4,0},{5,1},{6,2},{7,3},{8,12},{9,13},{10,... | collective-permute-start | bytes 196616 | tf_op jit(solution)/shard_map/ppermute | solution.py:34
  231.2 4.3 %collective-permute-start.35 = (bf16[32,1024]{1,0:T(8,128)(2,1)S(1)}, bf16[32,1024]{1,0:T(8,128)(2,1)S(1)}, u32[]{:S(2)}, u32[]{:S(2)}) collective-permute-start(bf16[32,1024]{1,0:T(8,128)(2,1)S(1)} %get-tuple-element.76), channel_id=1, source_target_pairs={{0,2},{1,3},{2,0},{3,1},{4,6},{5,7},{6,4},{7,5},{8,10},{9,11},{10,... | collective-permute-start | bytes 196616 | tf_op jit(solution)/shard_map/ppermute | solution.py:34
  234.1 30.5 %collective-permute-start.58 = (bf16[672,512]{1,0:T(8,128)(2,1)S(1)}, bf16[672,512]{1,0:T(8,128)(2,1)S(1)}, u32[]{:S(2)}, u32[]{:S(2)}) collective-permute-start(bf16[672,512]{1,0:T(8,128)(2,1)S(1)} %slice.362), channel_id=1, source_target_pairs={{0,4},{4,0},{8,12},{12,8},{16,20},{20,16},{24,28},{28,24},{1,5},{5... | collective-permute-start | bytes 2064392 | tf_op jit(solution)/shard_map/ppermute | solution.py:24
  235.4 1.5 collective-permute-start.43
  237.1 5.2 %collective-permute-start.46 = (bf16[32,1024]{1,0:T(8,128)(2,1)S(1)}, bf16[32,1024]{1,0:T(8,128)(2,1)S(1)}, u32[]{:S(2)}, u32[]{:S(2)}) collective-permute-start(bf16[32,1024]{1,0:T(8,128)(2,1)S(1)} %get-tuple-element.74), channel_id=1, source_target_pairs={{0,6},{1,7},{2,4},{3,5},{4,2},{5,3},{6,0},{7,1},{8,14},{9,15},{10,... | collective-permute-start | bytes 196616 | tf_op jit(solution)/shard_map/ppermute | solution.py:34
  238.9 16.3 %collective-permute-start.45 = (bf16[32,1024]{1,0:T(8,128)(2,1)S(1)}, bf16[32,1024]{1,0:T(8,128)(2,1)S(1)}, u32[]{:S(2)}, u32[]{:S(2)}) collective-permute-start(bf16[32,1024]{1,0:T(8,128)(2,1)S(1)} %get-tuple-element.75), channel_id=1, source_target_pairs={{0,4},{1,5},{2,6},{3,7},{4,0},{5,1},{6,2},{7,3},{8,12},{9,13},{10,... | collective-permute-start | bytes 196616 | tf_op jit(solution)/shard_map/ppermute | solution.py:34
  240.2 15.6 %collective-permute-start.44 = (bf16[32,1024]{1,0:T(8,128)(2,1)S(1)}, bf16[32,1024]{1,0:T(8,128)(2,1)S(1)}, u32[]{:S(2)}, u32[]{:S(2)}) collective-permute-start(bf16[32,1024]{1,0:T(8,128)(2,1)S(1)} %get-tuple-element.73), channel_id=1, source_target_pairs={{0,2},{1,3},{2,0},{3,1},{4,6},{5,7},{6,4},{7,5},{8,10},{9,11},{10,... | collective-permute-start | bytes 196616 | tf_op jit(solution)/shard_map/ppermute | solution.py:34
  240.7 34.8 %copy-start.6 = (f32[4096]{0:T(1024)S(1)}, f32[4096]{0:T(1024)}, u32[]{:S(2)}) copy-start(f32[4096]{0:T(1024)} %param.15) | copy-start | bytes 49156
  240.7 34.8 %copy-start.11 = (f32[32]{0:T(128)S(1)}, f32[32]{0:T(128)}, u32[]{:S(2)}) copy-start(f32[32]{0:T(128)} %copy-done.10) | copy-start | bytes 388
  242.3 25.0 %collective-permute-start.59 = (bf16[224,512]{1,0:T(8,128)(2,1)S(1)}, bf16[224,512]{1,0:T(8,128)(2,1)S(1)}, u32[]{:S(2)}, u32[]{:S(2)}) collective-permute-start(bf16[224,512]{1,0:T(8,128)(2,1)S(1)} %slice.363), channel_id=1, source_target_pairs={{0,4},{4,0},{8,12},{12,8},{16,20},{20,16},{24,28},{28,24},{1,5},{5... | collective-permute-start | bytes 688136 | tf_op jit(solution)/shard_map/ppermute | solution.py:24
  255.2 5.8 %collective-permute-start.38 = (bf16[32,1024]{1,0:T(8,128)(2,1)S(1)}, bf16[32,1024]{1,0:T(8,128)(2,1)S(1)}, u32[]{:S(2)}, u32[]{:S(2)}) collective-permute-start(bf16[32,1024]{1,0:T(8,128)(2,1)S(1)} %get-tuple-element.29), channel_id=1, source_target_pairs={{0,16},{4,20},{8,24},{12,28},{16,0},{20,4},{24,8},{28,12},{1,17},{... | collective-permute-start | bytes 196616 | tf_op jit(solution)/shard_map/ppermute | solution.py:18
  256.1 4.9 %collective-permute-start.51 = (f32[1024]{0:T(1024)S(1)}, f32[1024]{0:T(1024)S(1)}, u32[]{:S(2)}, u32[]{:S(2)}) collective-permute-start(f32[1024]{0:T(1024)S(1)} %add_add_fusion.1), channel_id=1, source_target_pairs={{0,1},{1,0},{2,3},{3,2},{4,5},{5,4},{6,7},{7,6},{8,9},{9,8},{10,11... | collective-permute-start | bytes 12296 | tf_op jit(solution)/shard_map/ppermute | solution.py:21
  261.0 4.6 %collective-permute-start.54 = (f32[1024]{0:T(1024)S(1)}, f32[1024]{0:T(1024)S(1)}, u32[]{:S(2)}, u32[]{:S(2)}) collective-permute-start(f32[1024]{0:T(1024)S(1)} %add.412), channel_id=1, source_target_pairs={{0,6},{1,7},{2,4},{3,5},{4,2},{5,3},{6,0},{7,1},{8,14},{9,15},{10,... | collective-permute-start | bytes 12296 | tf_op jit(solution)/shard_map/ppermute | solution.py:34
  263.5 3.6 %collective-permute-start.53 = (f32[1024]{0:T(1024)S(1)}, f32[1024]{0:T(1024)S(1)}, u32[]{:S(2)}, u32[]{:S(2)}) collective-permute-start(f32[1024]{0:T(1024)S(1)} %add.412), channel_id=1, source_target_pairs={{0,4},{1,5},{2,6},{3,7},{4,0},{5,1},{6,2},{7,3},{8,12},{9,13},{10,... | collective-permute-start | bytes 12296 | tf_op jit(solution)/shard_map/ppermute | solution.py:34
  263.6 3.6 %collective-permute-start.52 = (f32[1024]{0:T(1024)S(1)}, f32[1024]{0:T(1024)S(1)}, u32[]{:S(2)}, u32[]{:S(2)}) collective-permute-start(f32[1024]{0:T(1024)S(1)} %add.412), channel_id=1, source_target_pairs={{0,2},{1,3},{2,0},{3,1},{4,6},{5,7},{6,4},{7,5},{8,10},{9,11},{10,... | collective-permute-start | bytes 12296 | tf_op jit(solution)/shard_map/ppermute | solution.py:34
  267.3 4.5 %collective-permute-start.55 = (f32[1024]{0:T(1024)S(1)}, f32[1024]{0:T(1024)S(1)}, u32[]{:S(2)}, u32[]{:S(2)}) collective-permute-start(f32[1024]{0:T(1024)S(1)} %get-tuple-element.26), channel_id=1, source_target_pairs={{0,24},{4,28},{8,0},{12,4},{16,8},{20,12},{24,16},{28,20},{1,25},{... | collective-permute-start | bytes 12296 | tf_op jit(solution)/shard_map/ppermute | solution.py:18
  267.3 9.4 %copy-start.1 = (bf16[1792,512]{1,0:T(8,128)(2,1)}, bf16[1792,512]{1,0:T(8,128)(2,1)S(1)}, u32[]{:S(2)}) copy-start(bf16[1792,512]{1,0:T(8,128)(2,1)S(1)} %constant_dynamic-update-slice_fusion.14) | copy-start | bytes 5505028
  267.3 8.1 %collective-permute-start.47 = (bf16[32,1024]{1,0:T(8,128)(2,1)S(1)}, bf16[32,1024]{1,0:T(8,128)(2,1)S(1)}, u32[]{:S(2)}, u32[]{:S(2)}) collective-permute-start(bf16[32,1024]{1,0:T(8,128)(2,1)S(1)} %get-tuple-element.27), channel_id=1, source_target_pairs={{0,8},{4,12},{8,16},{12,20},{16,24},{20,28},{24,0},{28,4},{1,9},{5... | collective-permute-start | bytes 196616 | tf_op jit(solution)/shard_map/ppermute | solution.py:18
  269.4 4.5 %collective-permute-start.56 = (f32[1024]{0:T(1024)S(1)}, f32[1024]{0:T(1024)S(1)}, u32[]{:S(2)}, u32[]{:S(2)}) collective-permute-start(f32[1024]{0:T(1024)S(1)} %get-tuple-element.26), channel_id=1, source_target_pairs={{0,16},{4,20},{8,24},{12,28},{16,0},{20,4},{24,8},{28,12},{1,17},{... | collective-permute-start | bytes 12296 | tf_op jit(solution)/shard_map/ppermute | solution.py:18
  269.4 5.4 %collective-permute-start.57 = (f32[1024]{0:T(1024)S(1)}, f32[1024]{0:T(1024)S(1)}, u32[]{:S(2)}, u32[]{:S(2)}) collective-permute-start(f32[1024]{0:T(1024)S(1)} %get-tuple-element.26), channel_id=1, source_target_pairs={{0,8},{4,12},{8,16},{12,20},{16,24},{20,28},{24,0},{28,4},{1,9},{5... | collective-permute-start | bytes 12296 | tf_op jit(solution)/shard_map/ppermute | solution.py:18
  (8 other events, 16.6 us)
